TPU v7x, 32 devices: a whole 2x2x4 slice. The times are simulated.
32 devices in a mesh: frame: 4 (over z), height: 4 (over y, x), dp: 2 (over core).
Axes of the slice: x: 2, y: 2, z: 4, core: 2. Of those that a mesh axis runs over, the one named last changes fastest.
Arguments:
- clip_latents: bfloat16 [2, 8, 64, 16, 320], P('dp', 'frame', 'height'), may hold values from -6 to 6
- out_grad: bfloat16 [2, 8, 64, 16, 320], P('dp', 'frame', 'height'), may hold values from -6 to 6
- box_mask: int32 [2, 8, 64, 16], P('dp', 'frame', 'height'), may hold values from 0 to 1, as said below
- attn_weights: bfloat16 [1280, 320], replicated, may hold values from -0.3125 to 0.3125
- conv_weights: bfloat16 [2880, 320], replicated, may hold values from -0.109375 to 0.109375
- time_bias: float32 [5, 8, 8], replicated, may hold values from -4 to 250
Outputs:
- grad_input: bfloat16 [2, 8, 64, 16, 320], P('dp', 'frame', 'height')
- grad_attn: float32 [1280, 320], P(('frame', 'height', 'dp'))
- grad_conv: float32 [2880, 320], P(('height', 'dp'))
Inputs may be any that keep to these rules, and one draw needn't show every extreme that they name: Each frame of each clip has one grounding box: box_mask is 1 on a rectangle of 16 to 32 rows and 4 to 8 columns, 0 elsewhere.
All inputs are finite; a program needn't handle non-finite values.
Results may differ from a plain program's by a relative error of at most 0.025.
Values may be sent and summed in bfloat16 or wider, within the bound.
No kernel may reach another device: no remote copies, remote signals or barrier semaphores. Data moves between devices by JAX's collectives and lax.ppermute only.
A program may use at most 64 MiB of HBM per device.

v0:
```python
import functools

import jax
import jax.numpy as jnp
from jax import lax
from jax.experimental import pallas as pl
from jax.experimental.pallas import tpu as pltpu
from jax.sharding import PartitionSpec as P


ground_bias = 2.0
LANES = 128
BF = jnp.bfloat16
F32 = jnp.float32


def dot(left, right, dims=((1,), (0,))):
    return lax.dot_general(left, right, (dims, ((), ())), preferred_element_type=F32)


def is_pow2(count):
    return count & (count - 1) == 0


def peer(index, step, count):
    if is_pow2(count):
        return index ^ step
    return (step - index) % count


def trade(value, axis, step):
    count = lax.axis_size(axis)
    return lax.ppermute(value, axis, [(i, peer(i, step, count)) for i in range(count)])


def sigmoid(value):
    return 1.0 / (1.0 + jnp.exp(-value))


def merge_rows(value):
    return value.reshape(-1, value.shape[-1])


def head_tiles(channels, head_size):
    step = max(LANES, head_size)
    tiles = []
    for start in range(0, channels, step):
        width = min(step, channels - start)
        tiles.append((start, width, range(start // head_size, (start + width) // head_size)))
    return tiles


def head_mask(tokens, width, head_size, place):
    lane = lax.broadcasted_iota(jnp.int32, (tokens, width), 1)
    return lane // head_size == place


def stack_heads(tile, heads, head_size):
    if len(heads) == 1:
        return tile
    masks = [head_mask(*tile.shape, head_size, place) for place in range(len(heads))]
    return jnp.concatenate([tile * mask.astype(BF) for mask in masks], axis=0)


def pick_heads(stacked, heads, head_size):
    tokens = stacked.shape[0] // len(heads)
    result = stacked[:tokens]
    for place in range(1, len(heads)):
        mask = head_mask(tokens, stacked.shape[1], head_size, place)
        result = jnp.where(mask, stacked[place * tokens : (place + 1) * tokens], result)
    return result


def tile_of(ref, row, lanes):
    frames, _, cols, _ = ref.shape
    return ref[:, row, :, lanes].reshape(frames * cols, lanes.stop - lanes.start)


def forward_kernel(parts, channels, head_size, *refs):
    x_refs = refs[:parts]
    w_ref, bias_ref = refs[parts : parts + 2]
    q_ref, k_ref, v_ref, p_ref, o_ref, y_ref, a_ref, s_ref = refs[parts + 2 :]
    frames, rows, cols, _ = q_ref.shape
    tokens = frames * cols
    head_count = channels // head_size
    wide = jnp.concatenate([merge_rows(ref[...]) for ref in x_refs], axis=0)
    latents = wide[:, :channels]
    for place, ref in enumerate((q_ref, k_ref, v_ref)):
        block = slice(place * channels, (place + 1) * channels)
        part = dot(latents, w_ref[:, block], ((1,), (1,))).astype(BF)
        ref[...] = part.reshape(ref.shape)
    scaling = head_size ** (-0.5)
    spare = (channels // LANES) * LANES
    tile_row = lax.broadcasted_iota(jnp.int32, (LANES, tokens), 0)
    tile_col = lax.broadcasted_iota(jnp.int32, (LANES, tokens), 1)
    pick = jnp.where(tile_row - (channels - spare) == tile_col % cols, ground_bias, 0.0).astype(BF)
    marks = dot(wide[:, spare : spare + LANES], pick).reshape(frames, rows, cols, tokens)
    tiles = head_tiles(channels, head_size)
    for row in range(rows):
        for start, width, heads in tiles:
            lanes = slice(start, start + width)
            queries = stack_heads(tile_of(q_ref, row, lanes), heads, head_size)
            span = slice(heads[0] * tokens, (heads[-1] + 1) * tokens)
            s_ref[row, :, span] = dot(tile_of(k_ref, row, lanes), queries, ((1,), (1,)))
    for row in range(rows):
        mark = marks[:, row].reshape(tokens, tokens)
        for head in range(head_count):
            span = slice(head * tokens, (head + 1) * tokens)
            score = s_ref[row, :, span] * scaling + (bias_ref[:, span] + mark)
            score = jnp.exp(score - jnp.max(score, axis=0, keepdims=True))
            p_ref[row, :, span] = score * (1.0 / jnp.sum(score, axis=0, keepdims=True))
    for row in range(rows):
        for start, width, heads in tiles:
            lanes = slice(start, start + width)
            span = slice(heads[0] * tokens, (heads[-1] + 1) * tokens)
            out = dot(p_ref[row, :, span].astype(BF), tile_of(v_ref, row, lanes), ((0,), (0,)))
            mixed = pick_heads(out, heads, head_size).astype(BF)
            o_ref[:, row, :, lanes] = mixed.reshape(frames, cols, width)
    mixed = merge_rows(o_ref[...])
    residual = (latents.astype(F32) + dot(mixed, w_ref[:, 3 * channels :], ((1,), (1,)))).astype(BF)
    y_ref[...] = residual.reshape(y_ref.shape)
    value = residual.astype(F32)
    a_ref[...] = (value * sigmoid(value)).astype(BF).reshape(a_ref.shape)


def column_moves(me, dy_refs, edge_refs, move_ref, cols):
    blocks = []
    for ref, edge_ref in zip(dy_refs, edge_refs):
        edge = edge_ref[...]
        first = jnp.where(me == 0, edge, ref[:, :1])
        last = jnp.where(me == len(dy_refs) - 1, edge, ref[:, -1:])
        blocks.append(jnp.concatenate([first, ref[:, 1:-1], last], axis=1))
    whole = jnp.concatenate(blocks, axis=0)
    wide = merge_rows(whole).astype(F32)
    count = wide.shape[0]
    col = lax.broadcasted_iota(jnp.int32, wide.shape, 0) % cols
    left = jnp.where(col == cols - 1, 0.0, pltpu.roll(wide, count - 1, 0))
    right = jnp.where(col == 0, 0.0, pltpu.roll(wide, 1, 0))
    move_ref[0] = left.astype(BF).reshape(whole.shape)
    move_ref[1] = whole
    move_ref[2] = right.astype(BF).reshape(whole.shape)


def tap_of(moves, row_step, col_step, rows):
    return merge_rows(moves[col_step + 1, :, 1 - row_step : 1 - row_step + rows])


def write_blocks(total_ref, keep_ref, send_ref, place_ref, split, turn=False):
    if split is None:
        keep_ref[...] = total_ref[...].astype(BF)
        return
    frame_count, height_count, dp_count, size = split
    for step in range(height_count):
        for far in range(frame_count):
            owner = (place_ref[0] ^ far) if frame_count > 1 else 0
            owner = (owner * height_count + (place_ref[1] ^ step)) * dp_count
            for ref, side in ((keep_ref, place_ref[2]), (send_ref, 1 - place_ref[2])):
                first = pl.multiple_of((owner + side) * size, 8)
                block = total_ref[pl.ds(first, size), :]
                if turn:
                    ref[step] = block.T.astype(BF)
                else:
                    ref[step, far] = block.astype(BF)


def conv_grad_kernel(parts, grad_scale, split, *refs):
    place_ref = refs[0]
    dy_refs = refs[1 : 1 + parts]
    edge_refs = refs[1 + parts : 1 + 2 * parts]
    a_ref, keep_ref, send_ref, move_ref, total_ref = refs[1 + 2 * parts :]
    _, rows, cols, channels = a_ref.shape
    column_moves(place_ref[0], dy_refs, edge_refs, move_ref, cols)
    act = merge_rows(a_ref[...]).T
    for tap in range(9):
        moved = tap_of(move_ref, tap // 3 - 1, tap % 3 - 1, rows)
        total_ref[tap * channels : (tap + 1) * channels, :] = dot(act, moved) * grad_scale
    write_blocks(total_ref, keep_ref, send_ref, place_ref, split, turn=True)


def upstream_kernel(channels, grad_scale, *refs):
    moves, y_ref, o_ref, w_ref, conv_ref, g_ref, do_ref, mix_ref = refs
    rows = g_ref.shape[1]
    delta = None
    for tap in range(9):
        moved = tap_of(moves, tap // 3 - 1, tap % 3 - 1, rows)
        term = dot(moved, conv_ref[:, tap * channels : (tap + 1) * channels])
        delta = term if delta is None else delta + term
    value = merge_rows(y_ref[...]).astype(F32)
    sig = sigmoid(value)
    slope = sig * (1.0 + value * (1.0 - sig))
    dy = tap_of(moves, 0, 0, rows).astype(F32)
    upstream = (dy + slope * delta).astype(BF)
    g_ref[...] = upstream.reshape(g_ref.shape)
    back = dot(upstream, w_ref[:, 3 * channels :]).astype(BF)
    do_ref[...] = back.reshape(do_ref.shape)
    mix_ref[...] = dot(merge_rows(o_ref[...]).T, upstream) * grad_scale


def backward_kernel(parts, channels, head_size, grad_scale, split, *refs):
    place_ref = refs[0]
    x_refs = refs[1 : 1 + parts]
    (g_ref, do_ref, q_ref, k_ref, v_ref, p_ref, mix_ref, w_ref) = refs[1 + parts : 9 + parts]
    out_refs = refs[9 + parts : 9 + 2 * parts]
    keep_ref, send_ref, dq_ref, dk_ref, dv_ref, dp_ref, ds_ref, total_ref = refs[9 + 2 * parts :]
    frames, rows, cols, _ = q_ref.shape
    tokens = frames * cols
    scaling = head_size ** (-0.5)
    tiles = head_tiles(channels, head_size)
    for row in range(rows):
        for start, width, heads in tiles:
            lanes = slice(start, start + width)
            grads = stack_heads(tile_of(do_ref, row, lanes), heads, head_size)
            span = slice(heads[0] * tokens, (heads[-1] + 1) * tokens)
            dp_ref[row, :, span] = dot(tile_of(v_ref, row, lanes), grads, ((1,), (1,)))
    for row in range(rows):
        for head in range(channels // head_size):
            span = slice(head * tokens, (head + 1) * tokens)
            prob = p_ref[row, :, span]
            d_prob = dp_ref[row, :, span]
            row_dot = jnp.sum(prob * d_prob, axis=0, keepdims=True)
            ds_ref[row, :, span] = (prob * (d_prob - row_dot)).astype(BF)
    for row in range(rows):
        for start, width, heads in tiles:
            lanes = slice(start, start + width)
            span = slice(heads[0] * tokens, (heads[-1] + 1) * tokens)
            d_score = ds_ref[row, :, span]
            queries = stack_heads(tile_of(q_ref, row, lanes), heads, head_size)
            grads = stack_heads(tile_of(do_ref, row, lanes), heads, head_size)
            dq = pick_heads(dot(d_score, tile_of(k_ref, row, lanes), ((0,), (0,))), heads, head_size)
            dk = dot(d_score, queries)
            dv = dot(p_ref[row, :, span].astype(BF), grads)
            for ref, grad in ((dq_ref, dq * scaling), (dk_ref, dk * scaling), (dv_ref, dv)):
                ref[:, row, :, lanes] = grad.astype(BF).reshape(frames, cols, width)
    d_inputs = None
    for place, ref in enumerate((dq_ref, dk_ref, dv_ref)):
        block = slice(place * channels, (place + 1) * channels)
        term = dot(merge_rows(ref[...]), w_ref[:, block])
        d_inputs = term if d_inputs is None else d_inputs + term
    grads = (merge_rows(g_ref[...]).astype(F32) + d_inputs.astype(BF).astype(F32)).astype(BF)
    share = grads.shape[0] // parts
    for step, ref in enumerate(out_refs):
        ref[...] = grads[step * share : (step + 1) * share].reshape(ref.shape)
    latents = jnp.concatenate([merge_rows(ref[...])[:, :channels] for ref in x_refs], axis=0)
    turned = latents.T
    for place, ref in enumerate((dq_ref, dk_ref, dv_ref)):
        block = slice(place * channels, (place + 1) * channels)
        total_ref[block, :] = dot(turned, merge_rows(ref[...])) * grad_scale
    total_ref[3 * channels :, :] = mix_ref[...]
    write_blocks(total_ref, keep_ref, send_ref, place_ref, split)


def place_kernel(parts, *refs):
    place_ref = refs[0]
    part_refs = refs[1 : 1 + parts]
    out_ref = refs[1 + parts]
    rows = part_refs[0].shape[1]
    for step, ref in enumerate(part_refs):
        out_ref[:, pl.ds((place_ref[0] ^ step) * rows, rows)] = ref[...]


def prepare_kernel(parts, *refs):
    place_ref, x_hbm, mask_hbm, dy_hbm = refs[:4]
    x_refs = refs[4 : 4 + parts]
    dy_refs = refs[4 + parts : 4 + 2 * parts]
    edge_refs = refs[4 + 2 * parts : 4 + 3 * parts]
    x_ref, mask_ref, sems = refs[4 + 3 * parts :]
    frames, rows, cols, wide = x_refs[0].shape
    channels = x_ref.shape[-1]
    count = x_ref.shape[1]
    me = place_ref[0]
    moves = [(x_hbm, x_ref), (mask_hbm, mask_ref)]
    for step in range(parts):
        first = (me ^ step) * rows
        for source, size, to in (
            (first, rows, 1),
            (jnp.maximum(first - 1, 0), 1, 0),
            (jnp.minimum(first + rows, count - 1), 1, rows + 1),
        ):
            moves.append(
                (dy_hbm.at[:, pl.ds(source, size)], dy_refs[step].at[:, pl.ds(to, size)])
            )
        row = jnp.where(me == step, count - 1, 0)
        moves.append((dy_hbm.at[:, pl.ds(row, 1)], edge_refs[step]))
    copies = [
        pltpu.make_async_copy(source, target, sems.at[place])
        for place, (source, target) in enumerate(moves)
    ]
    for copy in copies:
        copy.start()
    for copy in copies[:2]:
        copy.wait()
    blank = jnp.zeros((1, wide - channels - cols), F32)
    for step, ref in enumerate(x_refs):
        first = (me ^ step) * rows
        ref[:, :, :, :channels] = x_ref[:, pl.ds(first, rows)]
        for frame in range(frames):
            for row in range(rows):
                line = mask_ref[frame, pl.ds(first + row, 1), :].astype(F32)
                spare = jnp.concatenate([line, blank], axis=1)
                spare = jnp.broadcast_to(spare, (cols, wide - channels))
                ref[frame, row, :, channels:] = spare.astype(BF)
    for copy in copies[2:]:
        copy.wait()


def bias_kernel(head_count, frame_count, cols, *refs):
    place_ref, time_hbm, w_hbm, bias_ref, w_ref, time_ref, sems = refs
    tokens = bias_ref.shape[0]
    all_frames = time_ref.shape[1]
    copies = [
        pltpu.make_async_copy(time_hbm, time_ref, sems.at[0]),
        pltpu.make_async_copy(w_hbm, w_ref, sems.at[1]),
    ]
    for copy in copies:
        copy.start()

    def product(left, right):
        return lax.dot_general(
            left,
            right,
            (((1,), (1,)), ((), ())),
            precision=lax.Precision.HIGHEST,
            preferred_element_type=F32,
        )

    def held(slot):
        far = (slot // (cols * frame_count)) ^ place_ref[0]
        return far * frame_count + (slot // cols) % frame_count

    def index(shape, axis):
        return lax.broadcasted_iota(jnp.int32, shape, axis)

    keys = (tokens, all_frames)
    one_hot = jnp.where(held(index(keys, 0)) == index(keys, 1), 1.0, 0.0).astype(F32)
    square = (tokens, tokens)
    same = index(square, 0) % cols == index(square, 1) % cols
    copies[0].wait()
    by_key = product(one_hot, time_ref[...].reshape(head_count * all_frames, all_frames))
    for head in range(head_count):
        part = by_key[:, head * all_frames : (head + 1) * all_frames]
        spread = jnp.where(same, product(part, one_hot), -1e30)
        bias_ref[:, head * tokens : (head + 1) * tokens] = spread
    copies[1].wait()


def pair_sum_kernel(*refs):
    left_ref, right_ref = refs[:2]
    for step, ref in enumerate(refs[2:]):
        ref[...] = (left_ref[step].astype(F32) + right_ref[step].astype(F32)).astype(BF)


def sum_of(refs):
    total = refs[0][...].astype(F32)
    for ref in refs[1:]:
        total = total + ref[...].astype(F32)
    return total


def spread_sum_kernel(count, *refs):
    total = sum_of(refs[:count])
    for step, ref in enumerate(refs[count:]):
        ref[...] = total[step].astype(ref.dtype)


def scatter_sum_kernel(count, *refs):
    place_ref = refs[0]
    out_refs = refs[1 + count : -1]
    total_ref = refs[-1]
    share = out_refs[0].shape[0]
    total = sum_of(refs[1 : 1 + count])
    if total.shape[0] < total_ref.shape[0]:
        total_ref[...] = jnp.zeros(total_ref.shape, F32)
    total_ref[: total.shape[0], :] = total
    for step, ref in enumerate(out_refs):
        first = pl.multiple_of((place_ref[0] ^ step) * share, 8)
        ref[...] = total_ref[pl.ds(first, share), :].astype(BF)


def plain_sum_kernel(*refs):
    refs[-1][...] = sum_of(refs[:-1]).astype(refs[-1].dtype)


def gather_kernel(parts, *refs):
    place_ref = refs[0]
    out_ref, total_ref = refs[1 + parts :]
    share = refs[1].shape[0]
    for step, ref in enumerate(refs[1 : 1 + parts]):
        first = pl.multiple_of((place_ref[0] ^ step) * share, 8)
        total_ref[pl.ds(first, share), :] = ref[...].astype(F32)
    out_ref[...] = total_ref[: out_ref.shape[0], :]


def call(kernel, outs, args, scratch=(), scalars=False, far=0, flops=0):
    vmem = pl.BlockSpec(memory_space=pltpu.VMEM)
    smem = pl.BlockSpec(memory_space=pltpu.SMEM)
    specs = [vmem] * len(args)
    if scalars:
        specs[0] = smem
    args = list(args)
    for index in range(1, 1 + far):
        specs[index] = pl.BlockSpec(memory_space=pltpu.MemorySpace.HBM)
        args[index] = pltpu.with_memory_space_constraint(args[index], pltpu.MemorySpace.HBM)
    moved = sum(v.size * v.dtype.itemsize for v in list(args) + list(outs))
    return pl.pallas_call(
        kernel,
        out_shape=outs,
        in_specs=specs,
        out_specs=[vmem] * len(outs),
        scratch_shapes=list(scratch),
        cost_estimate=pl.CostEstimate(flops=flops, transcendentals=0, bytes_accessed=moved),
        compiler_params=pltpu.CompilerParams(vmem_limit_bytes=16 * 1024 * 1024),
    )(*args)


def block_size(total, owners):
    size = total // owners
    return size if size % 8 == 0 else None


def pack_blocks(plain, frame_count, height_count, dp_count, me, high, side):
    blocks = plain.reshape(frame_count, height_count, dp_count, -1, plain.shape[-1])
    far = jnp.arange(frame_count) ^ (me if frame_count > 1 else 0)
    blocks = blocks[far][:, jnp.arange(height_count) ^ high]
    blocks = jnp.swapaxes(blocks, 0, 1)
    keep = lax.dynamic_index_in_dim(blocks, side, 2, keepdims=False)
    send = lax.dynamic_index_in_dim(blocks, 1 - side, 2, keepdims=False)
    return keep, send


def like(shape, dtype=BF):
    return jax.ShapeDtypeStruct(tuple(shape), dtype)


def whole_body(clip_latents, out_grad, box_mask, attn_weights, conv_weights, time_bias):
    clips, frame_count, row_count, cols, channels = clip_latents.shape
    head_count, all_frames, _ = time_bias.shape
    head_size = channels // head_count
    parts = lax.axis_size("frame")
    height_count = lax.axis_size("height")
    dp_count = lax.axis_size("dp")
    me = lax.axis_index("frame")
    high = lax.axis_index("height")
    side = lax.axis_index("dp")
    rows = row_count // parts
    assert clips == 1 and dp_count == 2 and rows * parts == row_count
    assert is_pow2(parts) and is_pow2(height_count)
    tokens = all_frames * cols
    pixels = tokens * rows
    place = jnp.stack([me, high, side]).astype(jnp.int32)

    def trades(values, axis):
        return [values[0]] + [
            trade(values[step], axis, step) for step in range(1, lax.axis_size(axis))
        ]

    x = clip_latents[0]
    dy = out_grad[0]
    spare = -channels % LANES
    assert cols <= spare
    wide = like((frame_count, rows, cols, channels + spare))
    blocks = call(
        functools.partial(prepare_kernel, parts),
        [wide] * parts
        + [like((frame_count, rows + 2, cols, channels))] * parts
        + [like((frame_count, 1, cols, channels))] * parts,
        [place, x, box_mask[0], dy],
        scratch=[
            pltpu.VMEM(x.shape, BF),
            pltpu.VMEM(box_mask.shape[1:], jnp.int32),
            pltpu.SemaphoreType.DMA((2 + 4 * parts,)),
        ],
        scalars=True,
        far=3,
    )
    x_parts = trades(blocks[:parts], "frame")

    last = parts - 1
    dy_parts = trades(blocks[parts : 2 * parts], "frame")
    edges = []
    for step in range(parts):
        pairs = []
        for i in range(height_count - 1):
            pairs.append((step * height_count + i, i + 1))
            pairs.append(((last ^ step) * height_count + i + 1, last * height_count + i))
        edges.append(lax.ppermute(blocks[2 * parts + step], ("frame", "height"), pairs))

    bias, attn_turned = call(
        functools.partial(bias_kernel, head_count, frame_count, cols),
        [like((tokens, head_count * tokens), F32), like((channels, 4 * channels))],
        [place, time_bias, attn_weights.T],
        scratch=[pltpu.VMEM(time_bias.shape, F32), pltpu.SemaphoreType.DMA((2,))],
        scalars=True,
        far=2,
    )

    half = like((all_frames, rows, cols, channels))
    square = (rows, tokens, head_count * tokens)
    q, k, v, p, o, y, a = call(
        functools.partial(forward_kernel, parts, channels, head_size),
        [half, half, half, like(square, F32), half, half, half],
        list(x_parts) + [attn_turned, bias],
        scratch=[pltpu.VMEM(square, F32)],
        flops=8 * pixels * channels * channels,
    )

    token_count = pixels * dp_count * parts * height_count
    grad_scale = float(token_count) ** (-0.5)

    def block_outs(total, frames, turn=False):
        size = block_size(total, frames * height_count * dp_count)
        if size is None:
            return None, [like((total, channels)), like((8, channels))]
        block = (channels, size) if turn else (frames, size, channels)
        shape = like((height_count,) + block)
        return (frames, height_count, dp_count, size), [shape, shape]

    def over_height(keep, send):
        got = lax.ppermute(send, "dp", [(0, 1), (1, 0)])
        both = call(pair_sum_kernel, [like(keep.shape[1:])] * height_count, [keep, got])
        return trades(both, "height")

    taps = conv_weights.shape[0]
    split, outs = block_outs(taps, 1, turn=True)
    keep, send, moves = call(
        functools.partial(conv_grad_kernel, parts, grad_scale, split),
        outs + [like((3, all_frames, rows + 2, cols, channels))],
        [place] + dy_parts + edges + [a],
        scratch=[pltpu.VMEM((taps, channels), F32)],
        scalars=True,
        flops=2 * pixels * taps * channels,
    )
    if split is None:
        keep, send = pack_blocks(keep, 1, height_count, dp_count, 0, high, side)
        keep, send = jnp.swapaxes(keep[:, 0], 1, 2), jnp.swapaxes(send[:, 0], 1, 2)
    conv_terms = over_height(keep, send)

    g, do, mix = call(
        functools.partial(upstream_kernel, channels, grad_scale),
        [half, half, like((channels, channels), F32)],
        [moves, y, o, attn_turned, conv_weights.T],
        flops=2 * pixels * taps * channels,
    )
    split, outs = block_outs(4 * channels, parts)
    piece = like((frame_count, rows, cols, channels))
    result = call(
        functools.partial(backward_kernel, parts, channels, head_size, grad_scale, split),
        [piece] * parts + outs,
        [place] + list(x_parts) + [g, do, q, k, v, p, mix, attn_turned],
        scratch=[pltpu.VMEM(half.shape, BF)] * 3
        + [pltpu.VMEM(square, F32), pltpu.VMEM(square, BF)]
        + [pltpu.VMEM((4 * channels, channels), F32)],
        scalars=True,
        flops=2 * pixels * taps * channels,
    )
    grad_parts = [result[0]]
    for step in range(1, parts):
        grad_parts.append(trade(result[step], "frame", step))
    keep, send = result[parts:]
    if split is None:
        keep, send = pack_blocks(keep, parts, height_count, dp_count, me, high, side)
    attn_terms = over_height(keep, send)
    shares = call(
        functools.partial(spread_sum_kernel, height_count),
        [like(keep.shape[2:])] * parts,
        attn_terms,
    )
    shares = trades(shares, "frame")
    grad_attn = call(plain_sum_kernel, [like(keep.shape[2:], F32)], shares)[0]

    size = conv_terms[0].shape[1]
    share = -(-channels // (parts * 8)) * 8
    shares = call(
        functools.partial(scatter_sum_kernel, height_count),
        [like((share, size))] * parts,
        [place] + conv_terms,
        scratch=[pltpu.VMEM((parts * share, size), F32)],
        scalars=True,
    )
    shares = trades(shares, "frame")
    mine = call(plain_sum_kernel, [like((share, size))], shares)[0]
    shares = trades([mine] * parts, "frame")
    grad_conv = call(
        functools.partial(gather_kernel, parts),
        [like((channels, size), F32)],
        [place] + shares,
        scratch=[pltpu.VMEM((parts * share, size), F32)],
        scalars=True,
    )[0].T
    grad_input = call(
        functools.partial(place_kernel, parts),
        [like((frame_count, row_count, cols, channels))],
        [place] + grad_parts,
        scalars=True,
    )[0]
    return (grad_input.reshape(clip_latents.shape), grad_attn, grad_conv)


def solution(mesh):
    in_specs = (
        P("dp", "frame", "height", None, None),
        P("dp", "frame", "height", None, None),
        P("dp", "frame", "height", None),
        P(),
        P(),
        P(),
    )
    out_specs = (
        P("dp", "frame", "height", None, None),
        P(("frame", "height", "dp"), None),
        P(("height", "dp"), None),
    )
    return jax.shard_map(whole_body, mesh=mesh, in_specs=in_specs, out_specs=out_specs, check_vma=False)
```

profile of v0, /device:TPU:0, one launch (start us, length us, event | category | flops | bytes accessed | tf_op | source)
XLA Modules:
  0.0 93.0 jit_solution(8255345086046691047)
XLA Ops:
  0.6 0.1 pad_add_fusion.refs_0_
  0.7 1.9 %shard_map.85 = (bf16[2,4,16,384]{3,2,1,0:T(8,128)(2,1)S(1)}, bf16[2,4,16,384]{3,2,1,0:T(8,128)(2,1)S(1)}, bf16[2,4,16,384]{3,2,1,0:T(8,128)(2,1)S(1)}, bf16[2,4...) custom-call(s32[3]{0:T(128)S(1)} %pad_add_fusion.refs_0_, ...), custom_call_target="tpu_custom_call" | custom-call | bytes 1624076 | tf_op jit(solution)/shard_map/pallas_call | solution.py:404
  2.7 3.1 %collective-permute-start = (bf16[2,4,16,384]{3,2,1,0:T(8,128)(2,1)S(1)}, bf16[2,4,16,384]{3,2,1,0:T(8,128)(2,1)S(1)}, u32[]{:S(2)}, u32[]{:S(2)}) collective-permute-start(bf16[2,4,16,384]{3,2,1,0:T(8,128)(2,1)S(1)} %get-tuple-element.53), channel_id=1, source_target_pairs={{0,8},{8,0},{16,24},{24,16},{1,9},{9,1},{17,25},{25,17},{2,10},{10... | collective-permute-start | bytes 294920 | tf_op jit(solution)/shard_map/ppermute | solution.py:33
  5.8 3.4 %collective-permute-start.6 = (bf16[2,1,16,320]{3,2,1,0:T(8,128)(2,1)S(1)}, bf16[2,1,16,320]{3,2,1,0:T(8,128)(2,1)S(1)}, u32[]{:S(2)}, u32[]{:S(2)}) collective-permute-start(bf16[2,1,16,320]{3,2,1,0:T(8,128)(2,1)S(1)} %get-tuple-element.60), channel_id=1, source_target_pairs={{0,2},{26,24},{2,4},{28,26},{4,6},{30,28},{1,3},{27,25},{3,5},{29,... | collective-permute-start | bytes 61448 | tf_op jit(solution)/shard_map/ppermute | solution.py:485
  9.2 0.7 collective-permute-start.7
  9.8 0.1 collective-permute-start.1
  9.9 6.5 %collective-permute-start.2 = (bf16[2,4,16,384]{3,2,1,0:T(8,128)(2,1)S(1)}, bf16[2,4,16,384]{3,2,1,0:T(8,128)(2,1)S(1)}, u32[]{:S(2)}, u32[]{:S(2)}) collective-permute-start(bf16[2,4,16,384]{3,2,1,0:T(8,128)(2,1)S(1)} %get-tuple-element.55), channel_id=1, source_target_pairs={{0,24},{8,16},{16,8},{24,0},{1,25},{9,17},{17,9},{25,1},{2,26},{10... | collective-permute-start | bytes 294920 | tf_op jit(solution)/shard_map/ppermute | solution.py:33
  16.5 0.6 collective-permute-start.4
  17.1 3.8 %collective-permute-start.5 = (bf16[2,6,16,320]{3,2,1,0:T(8,128)(2,1)S(1)}, bf16[2,6,16,320]{3,2,1,0:T(8,128)(2,1)S(1)}, u32[]{:S(2)}, u32[]{:S(2)}) collective-permute-start(bf16[2,6,16,320]{3,2,1,0:T(8,128)(2,1)S(1)} %get-tuple-element.59), channel_id=1, source_target_pairs={{0,24},{8,16},{16,8},{24,0},{1,25},{9,17},{17,9},{25,1},{2,26},{10... | collective-permute-start | bytes 368648 | tf_op jit(solution)/shard_map/ppermute | solution.py:33
  20.9 2.3 %shard_map.86 = (f32[128,640]{1,0:T(8,128)S(1)}, bf16[320,1280]{1,0:T(8,128)(2,1)S(1)}) custom-call(s32[3]{0:T(128)S(1)} %pad_add_fusion.refs_0_, f32[5,8,8]{2,1,0:T(8,128)} %refs_1_.1, bf16[320,1280]{1,0:T(8,128)(2,1)} %bitcast.11), custom_call_target="tpu_custom_call" | custom-call | bytes 1967372 | tf_op jit(solution)/shard_map/pallas_call | solution.py:404
  23.2 0.7 collective-permute-start.8
  23.9 0.7 collective-permute-start.9
  24.5 2.2 %shard_map.87 = (bf16[8,4,16,320]{3,2,1,0:T(8,128)(2,1)S(1)}, bf16[8,4,16,320]{3,2,1,0:T(8,128)(2,1)S(1)}, bf16[8,4,16,320]{3,2,1,0:T(8,128)(2,1)S(1)}, f32[4,12...) custom-call(bf16[2,4,16,384]{3,2,1,0:T(8,128)(2,1)S(1)} %get-tuple-e, ...), custom_call_target="tpu_custom_call" | custom-call | flops 419430400 | bytes 4816896 | tf_op jit(solution)/shard_map/pallas_call | solution.py:404
  26.8 5.4 %collective-permute-done.4.refs_3_ = bf16[2,6,16,320]{3,2,1,0:T(8,128)(2,1)S(1)} collective-permute-done((bf16[2,6,16,320]{3,2,1,0:T(8,128)(2,1)S(1)}, bf16[2,6,16,320]{3,2,1,0:T(8,128)(2,1)S(1)}, u32[]{:S(2)}, u32[]{:S(2)}) %collective-permute-start.4) | collective-permute-done | bytes 122912 | tf_op jit(solution)/shard_map/ppermute | solution.py:33
  32.2 3.1 %shard_map.88 = (bf16[4,320,360]{2,1,0:T(8,128)(2,1)S(1)}, bf16[4,320,360]{2,1,0:T(8,128)(2,1)S(1)}, bf16[3,8,6,16,320]{4,3,2,1,0:T(8,128)(2,1)S(1)}) custom-call(s32[3]{0:T(128)S(1)} %pad_add_fusion.refs_0_, bf16[2,6,16,320]{3,2,1,0:T(8,128)(2,1)S(1)} %get-tuple-element.56.refs_1_, bf16[2,6,16,320]{3,2,1,0:T(8,128)(2,1)S(1)} %collective-permute-done.3.refs_2_, ...), custom_call_target="tpu_custom_call" | custom-call | flops 943718400 | bytes 4218892 | tf_op jit(solution)/shard_map/pallas_call | solution.py:404
  35.3 0.1 collective-permute-start.20
  35.4 3.4 %shard_map.89 = (bf16[8,4,16,320]{3,2,1,0:T(8,128)(2,1)S(1)}, bf16[8,4,16,320]{3,2,1,0:T(8,128)(2,1)S(1)}, f32[320,320]{1,0:T(8,128)S(1)}) custom-call(bf16[3,8,6,16,320]{4,3,2,1,0:T(8,128)(2,1)S(1)} %get-tuple-element.67.refs_0_, bf16[8,4,16,320]{3,2,1,0:T(8,128)(2,1)S(1)} %get-tuple-element.68.refs_1_, ...), custom_call_target="tpu_custom_call" | custom-call | flops 943718400 | bytes 5857280 | tf_op jit(solution)/shard_map/pallas_call | solution.py:404
  38.7 3.0 %shard_map.90 = (bf16[2,4,16,320]{3,2,1,0:T(8,128)(2,1)S(1)}, bf16[2,4,16,320]{3,2,1,0:T(8,128)(2,1)S(1)}, bf16[2,4,16,320]{3,2,1,0:T(8,128)(2,1)S(1)}, bf16[2,4...) custom-call(s32[3]{0:T(128)S(1)} %pad_add_fusion.refs_0_, ...), custom_call_target="tpu_custom_call" | custom-call | flops 943718400 | bytes 5718028 | tf_op jit(solution)/shard_map/pallas_call | solution.py:404
  41.8 0.6 collective-permute-start.13
  42.4 0.2 shard_map.95
  42.6 4.8 %collective-permute-start.21 = (bf16[320,360]{1,0:T(8,128)(2,1)S(1)}, bf16[320,360]{1,0:T(8,128)(2,1)S(1)}, u32[]{:S(2)}, u32[]{:S(2)}) collective-permute-start(bf16[320,360]{1,0:T(8,128)(2,1)S(1)} %get-tuple-element.94), channel_id=1, source_target_pairs={{0,2},{2,0},{4,6},{6,4},{1,3},{3,1},{5,7},{7,5},{8,10},{10,8},{12,... | collective-permute-start | bytes 691208 | tf_op jit(solution)/shard_map/ppermute | solution.py:33
  47.4 2.2 %collective-permute-start.22 = (bf16[320,360]{1,0:T(8,128)(2,1)S(1)}, bf16[320,360]{1,0:T(8,128)(2,1)S(1)}, u32[]{:S(2)}, u32[]{:S(2)}) collective-permute-start(bf16[320,360]{1,0:T(8,128)(2,1)S(1)} %get-tuple-element.95), channel_id=1, source_target_pairs={{0,4},{2,6},{4,0},{6,2},{1,5},{3,7},{5,1},{7,3},{8,12},{10,14},{12... | collective-permute-start | bytes 691208 | tf_op jit(solution)/shard_map/ppermute | solution.py:33
  49.6 0.8 collective-permute-start.23
  50.4 3.8 %collective-permute-done.21.refs_2_ = bf16[320,360]{1,0:T(8,128)(2,1)S(1)} collective-permute-done((bf16[320,360]{1,0:T(8,128)(2,1)S(1)}, bf16[320,360]{1,0:T(8,128)(2,1)S(1)}, u32[]{:S(2)}, u32[]{:S(2)}) %collective-permute-start.21) | collective-permute-done | bytes 230432 | tf_op jit(solution)/shard_map/ppermute | solution.py:33
  54.2 5.8 %collective-permute-done.22.refs_3_ = bf16[320,360]{1,0:T(8,128)(2,1)S(1)} collective-permute-done((bf16[320,360]{1,0:T(8,128)(2,1)S(1)}, bf16[320,360]{1,0:T(8,128)(2,1)S(1)}, u32[]{:S(2)}, u32[]{:S(2)}) %collective-permute-start.22) | collective-permute-done | bytes 230432 | tf_op jit(solution)/shard_map/ppermute | solution.py:33
  60.0 1.6 %collective-permute-done.23.refs_4_ = bf16[320,360]{1,0:T(8,128)(2,1)S(1)} collective-permute-done((bf16[320,360]{1,0:T(8,128)(2,1)S(1)}, bf16[320,360]{1,0:T(8,128)(2,1)S(1)}, u32[]{:S(2)}, u32[]{:S(2)}) %collective-permute-start.23) | collective-permute-done | bytes 230432 | tf_op jit(solution)/shard_map/ppermute | solution.py:33
  61.5 0.7 shard_map.96
  62.3 0.1 collective-permute-start.24
  62.4 2.6 %collective-permute-start.25 = (bf16[80,360]{1,0:T(8,128)(2,1)S(1)}, bf16[80,360]{1,0:T(8,128)(2,1)S(1)}, u32[]{:S(2)}, u32[]{:S(2)}) collective-permute-start(bf16[80,360]{1,0:T(8,128)(2,1)S(1)} %get-tuple-element.99), channel_id=1, source_target_pairs={{0,16},{8,24},{16,0},{24,8},{1,17},{9,25},{17,1},{25,9},{2,18},{10... | collective-permute-start | bytes 172808 | tf_op jit(solution)/shard_map/ppermute | solution.py:33
  65.0 1.7 %collective-permute-start.26 = (bf16[80,360]{1,0:T(8,128)(2,1)S(1)}, bf16[80,360]{1,0:T(8,128)(2,1)S(1)}, u32[]{:S(2)}, u32[]{:S(2)}) collective-permute-start(bf16[80,360]{1,0:T(8,128)(2,1)S(1)} %get-tuple-element.100), channel_id=1, source_target_pairs={{0,24},{8,16},{16,8},{24,0},{1,25},{9,17},{17,9},{25,1},{2,26},{10... | collective-permute-start | bytes 172808 | tf_op jit(solution)/shard_map/ppermute | solution.py:33
  66.7 0.1 shard_map.92
  66.9 0.7 collective-permute-start.14
  67.6 1.7 %collective-permute-start.15 = (bf16[4,40,320]{2,1,0:T(8,128)(2,1)S(1)}, bf16[4,40,320]{2,1,0:T(8,128)(2,1)S(1)}, u32[]{:S(2)}, u32[]{:S(2)}) collective-permute-start(bf16[4,40,320]{2,1,0:T(8,128)(2,1)S(1)} %get-tuple-element.85), channel_id=1, source_target_pairs={{0,4},{2,6},{4,0},{6,2},{1,5},{3,7},{5,1},{7,3},{8,12},{10,14},{12... | collective-permute-start | bytes 307208 | tf_op jit(solution)/shard_map/ppermute | solution.py:33
  69.3 1.2 %collective-permute-start.16 = (bf16[4,40,320]{2,1,0:T(8,128)(2,1)S(1)}, bf16[4,40,320]{2,1,0:T(8,128)(2,1)S(1)}, u32[]{:S(2)}, u32[]{:S(2)}) collective-permute-start(bf16[4,40,320]{2,1,0:T(8,128)(2,1)S(1)} %get-tuple-element.86), channel_id=1, source_target_pairs={{0,6},{2,4},{4,2},{6,0},{1,7},{3,5},{5,3},{7,1},{8,14},{10,12},{12... | collective-permute-start | bytes 307208 | tf_op jit(solution)/shard_map/ppermute | solution.py:33
  70.5 0.9 collective-permute-done.26.refs_3_
  71.3 1.6 %collective-permute-start.12 = (bf16[2,4,16,320]{3,2,1,0:T(8,128)(2,1)S(1)}, bf16[2,4,16,320]{3,2,1,0:T(8,128)(2,1)S(1)}, u32[]{:S(2)}, u32[]{:S(2)}) collective-permute-start(bf16[2,4,16,320]{3,2,1,0:T(8,128)(2,1)S(1)} %get-tuple-element.80), channel_id=1, source_target_pairs={{0,24},{8,16},{16,8},{24,0},{1,25},{9,17},{17,9},{25,1},{2,26},{10... | collective-permute-start | bytes 245768 | tf_op jit(solution)/shard_map/ppermute | solution.py:33
  73.0 1.0 %collective-permute-start.27 = (bf16[80,360]{1,0:T(8,128)(2,1)S(1)}, bf16[80,360]{1,0:T(8,128)(2,1)S(1)}, u32[]{:S(2)}, u32[]{:S(2)}) collective-permute-start(bf16[80,360]{1,0:T(8,128)(2,1)S(1)} %shard_map.97.refs_1_), channel_id=1, source_target_pairs={{0,8},{8,0},{16,24},{24,16},{1,9},{9,1},{17,25},{25,17},{2,10},{10... | collective-permute-start | bytes 172808 | tf_op jit(solution)/shard_map/ppermute | solution.py:33
  74.1 1.8 %collective-permute-start.28 = (bf16[80,360]{1,0:T(8,128)(2,1)S(1)}, bf16[80,360]{1,0:T(8,128)(2,1)S(1)}, u32[]{:S(2)}, u32[]{:S(2)}) collective-permute-start(bf16[80,360]{1,0:T(8,128)(2,1)S(1)} %shard_map.97.refs_1_), channel_id=1, source_target_pairs={{0,16},{8,24},{16,0},{24,8},{1,17},{9,25},{17,1},{25,9},{2,18},{10... | collective-permute-start | bytes 172808 | tf_op jit(solution)/shard_map/ppermute | solution.py:33
  75.9 1.6 %collective-permute-start.29 = (bf16[80,360]{1,0:T(8,128)(2,1)S(1)}, bf16[80,360]{1,0:T(8,128)(2,1)S(1)}, u32[]{:S(2)}, u32[]{:S(2)}) collective-permute-start(bf16[80,360]{1,0:T(8,128)(2,1)S(1)} %shard_map.97.refs_1_), channel_id=1, source_target_pairs={{0,24},{8,16},{16,8},{24,0},{1,25},{9,17},{17,9},{25,1},{2,26},{10... | collective-permute-start | bytes 172808 | tf_op jit(solution)/shard_map/ppermute | solution.py:33
  77.5 0.1 shard_map.93
  77.6 2.8 %collective-permute-done.11.refs_3_ = bf16[2,4,16,320]{3,2,1,0:T(8,128)(2,1)S(1)} collective-permute-done((bf16[2,4,16,320]{3,2,1,0:T(8,128)(2,1)S(1)}, bf16[2,4,16,320]{3,2,1,0:T(8,128)(2,1)S(1)}, u32[]{:S(2)}, u32[]{:S(2)}) %collective-permute-start.11) | collective-permute-done | bytes 81952 | tf_op jit(solution)/shard_map/ppermute | solution.py:33
  80.4 4.4 %collective-permute-start.18 = (bf16[40,320]{1,0:T(8,128)(2,1)S(1)}, bf16[40,320]{1,0:T(8,128)(2,1)S(1)}, u32[]{:S(2)}, u32[]{:S(2)}) collective-permute-start(bf16[40,320]{1,0:T(8,128)(2,1)S(1)} %get-tuple-element.89), channel_id=1, source_target_pairs={{0,16},{8,24},{16,0},{24,8},{1,17},{9,25},{17,1},{25,9},{2,18},{10... | collective-permute-start | bytes 76808 | tf_op jit(solution)/shard_map/ppermute | solution.py:33
  84.8 0.4 collective-permute-done.17.refs_1_
  85.2 1.7 %collective-permute-start.19 = (bf16[40,320]{1,0:T(8,128)(2,1)S(1)}, bf16[40,320]{1,0:T(8,128)(2,1)S(1)}, u32[]{:S(2)}, u32[]{:S(2)}) collective-permute-start(bf16[40,320]{1,0:T(8,128)(2,1)S(1)} %get-tuple-element.90), channel_id=1, source_target_pairs={{0,24},{8,16},{16,8},{24,0},{1,25},{9,17},{17,9},{25,1},{2,26},{10... | collective-permute-start | bytes 76808 | tf_op jit(solution)/shard_map/ppermute | solution.py:33
  86.9 1.3 %shard_map.91 = bf16[2,16,16,320]{3,2,1,0:T(8,128)(2,1)} custom-call(s32[3]{0:T(128)S(1)} %pad_add_fusion.refs_0_, bf16[2,4,16,320]{3,2,1,0:T(8,128)(2,1)S(1)} %get-tuple-element.77.refs_1_, bf16[2,4,16,320]{3,2,1,0:T(8,128)(2,1)S(1)} %collective-permute-done.10.refs_2_, bf16[2,4,16,320]{3,2,1,0:T(8,128)(2,1)S(1)} %collective-permute-done.11.refs_3_, ...), custom_call_target="tpu_custom_call" | custom-call | bytes 655372 | tf_op jit(solution)/shard_map/pallas_call | solution.py:404
  88.2 2.7 %collective-permute-done.19.refs_3_ = bf16[40,320]{1,0:T(8,128)(2,1)S(1)} collective-permute-done((bf16[40,320]{1,0:T(8,128)(2,1)S(1)}, bf16[40,320]{1,0:T(8,128)(2,1)S(1)}, u32[]{:S(2)}, u32[]{:S(2)}) %collective-permute-start.19) | collective-permute-done | bytes 25632 | tf_op jit(solution)/shard_map/ppermute | solution.py:33
  90.9 0.6 shard_map.94
  91.6 1.4 %shard_map.98 = f32[320,360]{1,0:T(8,128)} custom-call(s32[3]{0:T(128)S(1)} %pad_add_fusion.refs_0_, bf16[80,360]{1,0:T(8,128)(2,1)S(1)} %shard_map.97.refs_1_, bf16[80,360]{1,0:T(8,128)(2,1)S(1)} %collective-permute-done.27.refs_2_, bf16[80,360]{1,0:T(8,128)(2,1)S(1)} %collective-permute-done.28.refs_3_, bf16[80,360]{1,0:T(8,128)(2,1)S(1)} %collective-permute-done.29.refs_4_), custom_call_target="tpu_custom_call" | custom-call | bytes 691212 | tf_op jit(solution)/shard_map/pallas_call | solution.py:404
  (29 shorter events, 0.1 us)
Async XLA Ops:
  2.7 14.4 %collective-permute-start = (bf16[2,4,16,384]{3,2,1,0:T(8,128)(2,1)S(1)}, bf16[2,4,16,384]{3,2,1,0:T(8,128)(2,1)S(1)}, u32[]{:S(2)}, u32[]{:S(2)}) collective-permute-start(bf16[2,4,16,384]{3,2,1,0:T(8,128)(2,1)S(1)} %get-tuple-element.53), channel_id=1, source_target_pairs={{0,8},{8,0},{16,24},{24,16},{1,9},{9,1},{17,25},{25,17},{2,10},{10... | collective-permute-start | bytes 294920 | tf_op jit(solution)/shard_map/ppermute | solution.py:33
  5.8 10.7 %collective-permute-start.6 = (bf16[2,1,16,320]{3,2,1,0:T(8,128)(2,1)S(1)}, bf16[2,1,16,320]{3,2,1,0:T(8,128)(2,1)S(1)}, u32[]{:S(2)}, u32[]{:S(2)}) collective-permute-start(bf16[2,1,16,320]{3,2,1,0:T(8,128)(2,1)S(1)} %get-tuple-element.60), channel_id=1, source_target_pairs={{0,2},{26,24},{2,4},{28,26},{4,6},{30,28},{1,3},{27,25},{3,5},{29,... | collective-permute-start | bytes 61448 | tf_op jit(solution)/shard_map/ppermute | solution.py:485
  9.2 7.3 %collective-permute-start.7 = (bf16[2,1,16,320]{3,2,1,0:T(8,128)(2,1)S(1)}, bf16[2,1,16,320]{3,2,1,0:T(8,128)(2,1)S(1)}, u32[]{:S(2)}, u32[]{:S(2)}) collective-permute-start(bf16[2,1,16,320]{3,2,1,0:T(8,128)(2,1)S(1)} %get-tuple-element.61), channel_id=1, source_target_pairs={{8,2},{18,24},{10,4},{20,26},{12,6},{22,28},{9,3},{19,25},{11,5},{... | collective-permute-start | bytes 61448 | tf_op jit(solution)/shard_map/ppermute | solution.py:485
  9.8 13.3 %collective-permute-start.1 = (bf16[2,4,16,384]{3,2,1,0:T(8,128)(2,1)S(1)}, bf16[2,4,16,384]{3,2,1,0:T(8,128)(2,1)S(1)}, u32[]{:S(2)}, u32[]{:S(2)}) collective-permute-start(bf16[2,4,16,384]{3,2,1,0:T(8,128)(2,1)S(1)} %get-tuple-element.54), channel_id=1, source_target_pairs={{0,16},{8,24},{16,0},{24,8},{1,17},{9,25},{17,1},{25,9},{2,18},{10... | collective-permute-start | bytes 294920 | tf_op jit(solution)/shard_map/ppermute | solution.py:33
  9.9 13.9 %collective-permute-start.2 = (bf16[2,4,16,384]{3,2,1,0:T(8,128)(2,1)S(1)}, bf16[2,4,16,384]{3,2,1,0:T(8,128)(2,1)S(1)}, u32[]{:S(2)}, u32[]{:S(2)}) collective-permute-start(bf16[2,4,16,384]{3,2,1,0:T(8,128)(2,1)S(1)} %get-tuple-element.55), channel_id=1, source_target_pairs={{0,24},{8,16},{16,8},{24,0},{1,25},{9,17},{17,9},{25,1},{2,26},{10... | collective-permute-start | bytes 294920 | tf_op jit(solution)/shard_map/ppermute | solution.py:33
  16.5 10.3 %collective-permute-start.3 = (bf16[2,6,16,320]{3,2,1,0:T(8,128)(2,1)S(1)}, bf16[2,6,16,320]{3,2,1,0:T(8,128)(2,1)S(1)}, u32[]{:S(2)}, u32[]{:S(2)}) collective-permute-start(bf16[2,6,16,320]{3,2,1,0:T(8,128)(2,1)S(1)} %get-tuple-element.57), channel_id=1, source_target_pairs={{0,8},{8,0},{16,24},{24,16},{1,9},{9,1},{17,25},{25,17},{2,10},{10... | collective-permute-start | bytes 368648 | tf_op jit(solution)/shard_map/ppermute | solution.py:33
  16.5 15.7 %collective-permute-start.4 = (bf16[2,6,16,320]{3,2,1,0:T(8,128)(2,1)S(1)}, bf16[2,6,16,320]{3,2,1,0:T(8,128)(2,1)S(1)}, u32[]{:S(2)}, u32[]{:S(2)}) collective-permute-start(bf16[2,6,16,320]{3,2,1,0:T(8,128)(2,1)S(1)} %get-tuple-element.58), channel_id=1, source_target_pairs={{0,16},{8,24},{16,0},{24,8},{1,17},{9,25},{17,1},{25,9},{2,18},{10... | collective-permute-start | bytes 368648 | tf_op jit(solution)/shard_map/ppermute | solution.py:33
  17.1 15.1 %collective-permute-start.5 = (bf16[2,6,16,320]{3,2,1,0:T(8,128)(2,1)S(1)}, bf16[2,6,16,320]{3,2,1,0:T(8,128)(2,1)S(1)}, u32[]{:S(2)}, u32[]{:S(2)}) collective-permute-start(bf16[2,6,16,320]{3,2,1,0:T(8,128)(2,1)S(1)} %get-tuple-element.59), channel_id=1, source_target_pairs={{0,24},{8,16},{16,8},{24,0},{1,25},{9,17},{17,9},{25,1},{2,26},{10... | collective-permute-start | bytes 368648 | tf_op jit(solution)/shard_map/ppermute | solution.py:33
  23.2 3.5 %collective-permute-start.8 = (bf16[2,1,16,320]{3,2,1,0:T(8,128)(2,1)S(1)}, bf16[2,1,16,320]{3,2,1,0:T(8,128)(2,1)S(1)}, u32[]{:S(2)}, u32[]{:S(2)}) collective-permute-start(bf16[2,1,16,320]{3,2,1,0:T(8,128)(2,1)S(1)} %get-tuple-element.62), channel_id=1, source_target_pairs={{16,2},{10,24},{18,4},{12,26},{20,6},{14,28},{17,3},{11,25},{19,5}... | collective-permute-start | bytes 61448 | tf_op jit(solution)/shard_map/ppermute | solution.py:485
  23.9 2.9 %collective-permute-start.9 = (bf16[2,1,16,320]{3,2,1,0:T(8,128)(2,1)S(1)}, bf16[2,1,16,320]{3,2,1,0:T(8,128)(2,1)S(1)}, u32[]{:S(2)}, u32[]{:S(2)}) collective-permute-start(bf16[2,1,16,320]{3,2,1,0:T(8,128)(2,1)S(1)} %get-tuple-element.63), channel_id=1, source_target_pairs={{24,2},{2,24},{26,4},{4,26},{28,6},{6,28},{25,3},{3,25},{27,5},{5,... | collective-permute-start | bytes 61448 | tf_op jit(solution)/shard_map/ppermute | solution.py:485
  26.7 8.6 %copy-start = (bf16[2880,320]{0,1:T(8,128)(2,1)S(1)}, bf16[2880,320]{0,1:T(8,128)(2,1)}, u32[]{:S(2)}) copy-start(bf16[2880,320]{0,1:T(8,128)(2,1)} %param.10) | copy-start | bytes 5529604
  35.3 7.1 %collective-permute-start.20 = (bf16[4,320,360]{2,1,0:T(8,128)(2,1)S(1)}, bf16[4,320,360]{2,1,0:T(8,128)(2,1)S(1)}, u32[]{:S(2)}, u32[]{:S(2)}) collective-permute-start(bf16[4,320,360]{2,1,0:T(8,128)(2,1)S(1)} %get-tuple-element.92), channel_id=1, source_target_pairs={{0,1},{1,0},{2,3},{3,2},{4,5},{5,4},{6,7},{7,6},{8,9},{9,8},{10,11... | collective-permute-start | bytes 2764808 | tf_op jit(solution)/shard_map/ppermute | solution.py:518
  41.8 25.0 %collective-permute-start.13 = (bf16[4,4,40,320]{3,2,1,0:T(8,128)(2,1)S(1)}, bf16[4,4,40,320]{3,2,1,0:T(8,128)(2,1)S(1)}, u32[]{:S(2)}, u32[]{:S(2)}) collective-permute-start(bf16[4,4,40,320]{3,2,1,0:T(8,128)(2,1)S(1)} %get-tuple-element.82), channel_id=1, source_target_pairs={{0,1},{1,0},{2,3},{3,2},{4,5},{5,4},{6,7},{7,6},{8,9},{9,8},{10,11... | collective-permute-start | bytes 1228808 | tf_op jit(solution)/shard_map/ppermute | solution.py:518
  42.6 11.6 %collective-permute-start.21 = (bf16[320,360]{1,0:T(8,128)(2,1)S(1)}, bf16[320,360]{1,0:T(8,128)(2,1)S(1)}, u32[]{:S(2)}, u32[]{:S(2)}) collective-permute-start(bf16[320,360]{1,0:T(8,128)(2,1)S(1)} %get-tuple-element.94), channel_id=1, source_target_pairs={{0,2},{2,0},{4,6},{6,4},{1,3},{3,1},{5,7},{7,5},{8,10},{10,8},{12,... | collective-permute-start | bytes 691208 | tf_op jit(solution)/shard_map/ppermute | solution.py:33
  47.4 12.6 %collective-permute-start.22 = (bf16[320,360]{1,0:T(8,128)(2,1)S(1)}, bf16[320,360]{1,0:T(8,128)(2,1)S(1)}, u32[]{:S(2)}, u32[]{:S(2)}) collective-permute-start(bf16[320,360]{1,0:T(8,128)(2,1)S(1)} %get-tuple-element.95), channel_id=1, source_target_pairs={{0,4},{2,6},{4,0},{6,2},{1,5},{3,7},{5,1},{7,3},{8,12},{10,14},{12... | collective-permute-start | bytes 691208 | tf_op jit(solution)/shard_map/ppermute | solution.py:33
  49.6 11.9 %collective-permute-start.23 = (bf16[320,360]{1,0:T(8,128)(2,1)S(1)}, bf16[320,360]{1,0:T(8,128)(2,1)S(1)}, u32[]{:S(2)}, u32[]{:S(2)}) collective-permute-start(bf16[320,360]{1,0:T(8,128)(2,1)S(1)} %get-tuple-element.96), channel_id=1, source_target_pairs={{0,6},{2,4},{4,2},{6,0},{1,7},{3,5},{5,3},{7,1},{8,14},{10,12},{12... | collective-permute-start | bytes 691208 | tf_op jit(solution)/shard_map/ppermute | solution.py:33
  50.4 17.2 %collective-permute-start.10 = (bf16[2,4,16,320]{3,2,1,0:T(8,128)(2,1)S(1)}, bf16[2,4,16,320]{3,2,1,0:T(8,128)(2,1)S(1)}, u32[]{:S(2)}, u32[]{:S(2)}) collective-permute-start(bf16[2,4,16,320]{3,2,1,0:T(8,128)(2,1)S(1)} %get-tuple-element.78), channel_id=1, source_target_pairs={{0,8},{8,0},{16,24},{24,16},{1,9},{9,1},{17,25},{25,17},{2,10},{10... | collective-permute-start | bytes 245768 | tf_op jit(solution)/shard_map/ppermute | solution.py:33
  62.3 7.0 %collective-permute-start.24 = (bf16[80,360]{1,0:T(8,128)(2,1)S(1)}, bf16[80,360]{1,0:T(8,128)(2,1)S(1)}, u32[]{:S(2)}, u32[]{:S(2)}) collective-permute-start(bf16[80,360]{1,0:T(8,128)(2,1)S(1)} %get-tuple-element.98), channel_id=1, source_target_pairs={{0,8},{8,0},{16,24},{24,16},{1,9},{9,1},{17,25},{25,17},{2,10},{10... | collective-permute-start | bytes 172808 | tf_op jit(solution)/shard_map/ppermute | solution.py:33
  62.4 8.1 %collective-permute-start.25 = (bf16[80,360]{1,0:T(8,128)(2,1)S(1)}, bf16[80,360]{1,0:T(8,128)(2,1)S(1)}, u32[]{:S(2)}, u32[]{:S(2)}) collective-permute-start(bf16[80,360]{1,0:T(8,128)(2,1)S(1)} %get-tuple-element.99), channel_id=1, source_target_pairs={{0,16},{8,24},{16,0},{24,8},{1,17},{9,25},{17,1},{25,9},{2,18},{10... | collective-permute-start | bytes 172808 | tf_op jit(solution)/shard_map/ppermute | solution.py:33
  65.0 6.3 %collective-permute-start.26 = (bf16[80,360]{1,0:T(8,128)(2,1)S(1)}, bf16[80,360]{1,0:T(8,128)(2,1)S(1)}, u32[]{:S(2)}, u32[]{:S(2)}) collective-permute-start(bf16[80,360]{1,0:T(8,128)(2,1)S(1)} %get-tuple-element.100), channel_id=1, source_target_pairs={{0,24},{8,16},{16,8},{24,0},{1,25},{9,17},{17,9},{25,1},{2,26},{10... | collective-permute-start | bytes 172808 | tf_op jit(solution)/shard_map/ppermute | solution.py:33
  66.9 6.1 %collective-permute-start.14 = (bf16[4,40,320]{2,1,0:T(8,128)(2,1)S(1)}, bf16[4,40,320]{2,1,0:T(8,128)(2,1)S(1)}, u32[]{:S(2)}, u32[]{:S(2)}) collective-permute-start(bf16[4,40,320]{2,1,0:T(8,128)(2,1)S(1)} %get-tuple-element.84), channel_id=1, source_target_pairs={{0,2},{2,0},{4,6},{6,4},{1,3},{3,1},{5,7},{7,5},{8,10},{10,8},{12,... | collective-permute-start | bytes 307208 | tf_op jit(solution)/shard_map/ppermute | solution.py:33
  67.6 6.5 %collective-permute-start.15 = (bf16[4,40,320]{2,1,0:T(8,128)(2,1)S(1)}, bf16[4,40,320]{2,1,0:T(8,128)(2,1)S(1)}, u32[]{:S(2)}, u32[]{:S(2)}) collective-permute-start(bf16[4,40,320]{2,1,0:T(8,128)(2,1)S(1)} %get-tuple-element.85), channel_id=1, source_target_pairs={{0,4},{2,6},{4,0},{6,2},{1,5},{3,7},{5,1},{7,3},{8,12},{10,14},{12... | collective-permute-start | bytes 307208 | tf_op jit(solution)/shard_map/ppermute | solution.py:33
  69.3 6.6 %collective-permute-start.16 = (bf16[4,40,320]{2,1,0:T(8,128)(2,1)S(1)}, bf16[4,40,320]{2,1,0:T(8,128)(2,1)S(1)}, u32[]{:S(2)}, u32[]{:S(2)}) collective-permute-start(bf16[4,40,320]{2,1,0:T(8,128)(2,1)S(1)} %get-tuple-element.86), channel_id=1, source_target_pairs={{0,6},{2,4},{4,2},{6,0},{1,7},{3,5},{5,3},{7,1},{8,14},{10,12},{12... | collective-permute-start | bytes 307208 | tf_op jit(solution)/shard_map/ppermute | solution.py:33
  70.4 9.9 %collective-permute-start.11 = (bf16[2,4,16,320]{3,2,1,0:T(8,128)(2,1)S(1)}, bf16[2,4,16,320]{3,2,1,0:T(8,128)(2,1)S(1)}, u32[]{:S(2)}, u32[]{:S(2)}) collective-permute-start(bf16[2,4,16,320]{3,2,1,0:T(8,128)(2,1)S(1)} %get-tuple-element.79), channel_id=1, source_target_pairs={{0,16},{8,24},{16,0},{24,8},{1,17},{9,25},{17,1},{25,9},{2,18},{10... | collective-permute-start | bytes 245768 | tf_op jit(solution)/shard_map/ppermute | solution.py:33
  71.3 9.1 %collective-permute-start.12 = (bf16[2,4,16,320]{3,2,1,0:T(8,128)(2,1)S(1)}, bf16[2,4,16,320]{3,2,1,0:T(8,128)(2,1)S(1)}, u32[]{:S(2)}, u32[]{:S(2)}) collective-permute-start(bf16[2,4,16,320]{3,2,1,0:T(8,128)(2,1)S(1)} %get-tuple-element.80), channel_id=1, source_target_pairs={{0,24},{8,16},{16,8},{24,0},{1,25},{9,17},{17,9},{25,1},{2,26},{10... | collective-permute-start | bytes 245768 | tf_op jit(solution)/shard_map/ppermute | solution.py:33
  73.0 18.5 %collective-permute-start.27 = (bf16[80,360]{1,0:T(8,128)(2,1)S(1)}, bf16[80,360]{1,0:T(8,128)(2,1)S(1)}, u32[]{:S(2)}, u32[]{:S(2)}) collective-permute-start(bf16[80,360]{1,0:T(8,128)(2,1)S(1)} %shard_map.97.refs_1_), channel_id=1, source_target_pairs={{0,8},{8,0},{16,24},{24,16},{1,9},{9,1},{17,25},{25,17},{2,10},{10... | collective-permute-start | bytes 172808 | tf_op jit(solution)/shard_map/ppermute | solution.py:33
  74.1 17.5 %collective-permute-start.28 = (bf16[80,360]{1,0:T(8,128)(2,1)S(1)}, bf16[80,360]{1,0:T(8,128)(2,1)S(1)}, u32[]{:S(2)}, u32[]{:S(2)}) collective-permute-start(bf16[80,360]{1,0:T(8,128)(2,1)S(1)} %shard_map.97.refs_1_), channel_id=1, source_target_pairs={{0,16},{8,24},{16,0},{24,8},{1,17},{9,25},{17,1},{25,9},{2,18},{10... | collective-permute-start | bytes 172808 | tf_op jit(solution)/shard_map/ppermute | solution.py:33
  75.9 15.7 %collective-permute-start.29 = (bf16[80,360]{1,0:T(8,128)(2,1)S(1)}, bf16[80,360]{1,0:T(8,128)(2,1)S(1)}, u32[]{:S(2)}, u32[]{:S(2)}) collective-permute-start(bf16[80,360]{1,0:T(8,128)(2,1)S(1)} %shard_map.97.refs_1_), channel_id=1, source_target_pairs={{0,24},{8,16},{16,8},{24,0},{1,25},{9,17},{17,9},{25,1},{2,26},{10... | collective-permute-start | bytes 172808 | tf_op jit(solution)/shard_map/ppermute | solution.py:33
  80.4 4.8 %collective-permute-start.17 = (bf16[40,320]{1,0:T(8,128)(2,1)S(1)}, bf16[40,320]{1,0:T(8,128)(2,1)S(1)}, u32[]{:S(2)}, u32[]{:S(2)}) collective-permute-start(bf16[40,320]{1,0:T(8,128)(2,1)S(1)} %get-tuple-element.88), channel_id=1, source_target_pairs={{0,8},{8,0},{16,24},{24,16},{1,9},{9,1},{17,25},{25,17},{2,10},{10... | collective-permute-start | bytes 76808 | tf_op jit(solution)/shard_map/ppermute | solution.py:33
  80.4 7.8 %collective-permute-start.18 = (bf16[40,320]{1,0:T(8,128)(2,1)S(1)}, bf16[40,320]{1,0:T(8,128)(2,1)S(1)}, u32[]{:S(2)}, u32[]{:S(2)}) collective-permute-start(bf16[40,320]{1,0:T(8,128)(2,1)S(1)} %get-tuple-element.89), channel_id=1, source_target_pairs={{0,16},{8,24},{16,0},{24,8},{1,17},{9,25},{17,1},{25,9},{2,18},{10... | collective-permute-start | bytes 76808 | tf_op jit(solution)/shard_map/ppermute | solution.py:33
  85.2 5.7 %collective-permute-start.19 = (bf16[40,320]{1,0:T(8,128)(2,1)S(1)}, bf16[40,320]{1,0:T(8,128)(2,1)S(1)}, u32[]{:S(2)}, u32[]{:S(2)}) collective-permute-start(bf16[40,320]{1,0:T(8,128)(2,1)S(1)} %get-tuple-element.90), channel_id=1, source_target_pairs={{0,24},{8,16},{16,8},{24,0},{1,25},{9,17},{17,9},{25,1},{2,26},{10... | collective-permute-start | bytes 76808 | tf_op jit(solution)/shard_map/ppermute | solution.py:33
where the time goes:
time: 93.2 us; the launch traced here: 93 us
  starting transfers between devices  48.1 us (52%)
  waiting for transfers between devices  23.5 us (25%)
  Pallas kernels  20.5 us (22%)
    ppermute x24, starting transfers between devices, trade(): lax.ppermute(value, axis, [(i, peer(i, step, count)) for i in range(count)])  42.1 us
    ppermute x24, waiting for transfers between devices, trade(): lax.ppermute(value, axis, [(i, peer(i, step, count)) for i in range(count)])  23.5 us
    pallas_call x14, Pallas kernels, call(): pl.pallas_call(kernel, out_shape=outs, in_specs=specs, out_specs=[vmem] *...  20.5 us
    ppermute x4, starting transfers between devices, whole_body(): lax.ppermute(blocks[2 * parts + step], ('frame', 'height'), pairs)  5.37 us
  transfers between devices with their start and end apart: 30, of which 8 were waited for; matrix products, arithmetic and copies ran while one was open for 0% of the time, Pallas kernels for 15%

commit v1 on v0

--- a/solution.py
+++ b/solution.py
@@ -39,6 +39,38 @@
 
 def merge_rows(value):
     return value.reshape(-1, value.shape[-1])
+
+
+def up_to(count, unit):
+    return -(-count // unit) * unit
+
+
+def packed_rows(count, channels):
+    whole, rest = divmod(channels, LANES)
+    assert rest <= LANES // 2 and count % 32 == 0
+    return count * whole + (count // 2 if rest else 0)
+
+
+def pack(ref, value):
+    count, channels = value.shape
+    whole, rest = divmod(channels, LANES)
+    for tile in range(whole):
+        ref[tile * count : (tile + 1) * count, :] = value[:, tile * LANES : (tile + 1) * LANES]
+    if rest:
+        half = count // 2
+        sides = [value[:half, whole * LANES :], value[half:, whole * LANES :]]
+        if 2 * rest < LANES:
+            sides.append(jnp.zeros((half, LANES - 2 * rest), value.dtype))
+        ref[whole * count : whole * count + half, :] = jnp.concatenate(sides, axis=1)
+
+
+def unpack(ref, count, channels):
+    whole, rest = divmod(channels, LANES)
+    tiles = [ref[tile * count : (tile + 1) * count, :] for tile in range(whole)]
+    if rest:
+        half = ref[whole * count : whole * count + count // 2, :]
+        tiles.append(jnp.concatenate([half[:, :rest], half[:, rest : 2 * rest]], axis=0))
+    return jnp.concatenate(tiles, axis=1)
 
 
 def head_tiles(channels, head_size):
@@ -79,22 +111,28 @@
 def forward_kernel(parts, channels, head_size, *refs):
     x_refs = refs[:parts]
     w_ref, bias_ref = refs[parts : parts + 2]
-    q_ref, k_ref, v_ref, p_ref, o_ref, y_ref, a_ref, s_ref = refs[parts + 2 :]
+    x_ref, q_ref, k_ref, v_ref, p_ref, o_ref, y_ref, a_ref, s_ref = refs[parts + 2 :]
     frames, rows, cols, _ = q_ref.shape
     tokens = frames * cols
     head_count = channels // head_size
-    wide = jnp.concatenate([merge_rows(ref[...]) for ref in x_refs], axis=0)
-    latents = wide[:, :channels]
+    count = tokens * rows // parts
+    at = packed_rows(count, channels)
+    lines = x_refs[0].shape[0] - at
+    latents = jnp.concatenate([unpack(ref, count, channels) for ref in x_refs], axis=0)
+    x_ref[...] = latents.reshape(x_ref.shape)
     for place, ref in enumerate((q_ref, k_ref, v_ref)):
         block = slice(place * channels, (place + 1) * channels)
         part = dot(latents, w_ref[:, block], ((1,), (1,))).astype(BF)
         ref[...] = part.reshape(ref.shape)
     scaling = head_size ** (-0.5)
-    spare = (channels // LANES) * LANES
-    tile_row = lax.broadcasted_iota(jnp.int32, (LANES, tokens), 0)
-    tile_col = lax.broadcasted_iota(jnp.int32, (LANES, tokens), 1)
-    pick = jnp.where(tile_row - (channels - spare) == tile_col % cols, ground_bias, 0.0).astype(BF)
-    marks = dot(wide[:, spare : spare + LANES], pick).reshape(frames, rows, cols, tokens)
+    held = jnp.concatenate([ref[at:, :] for ref in x_refs], axis=0)
+    lane = lax.broadcasted_iota(jnp.int32, (LANES, tokens), 0)
+    column = lax.broadcasted_iota(jnp.int32, (LANES, tokens), 1)
+    held = dot(held, jnp.where(lane == column % cols, ground_bias, 0.0).astype(BF)).astype(BF)
+    token = lax.broadcasted_iota(jnp.int32, (tokens, parts * lines), 0) // cols
+    line = lax.broadcasted_iota(jnp.int32, (tokens, parts * lines), 1)
+    part_frames = frames // parts
+    first_line = (token // part_frames) * lines + (token % part_frames) * rows
     tiles = head_tiles(channels, head_size)
     for row in range(rows):
         for start, width, heads in tiles:
@@ -103,7 +141,7 @@
             span = slice(heads[0] * tokens, (heads[-1] + 1) * tokens)
             s_ref[row, :, span] = dot(tile_of(k_ref, row, lanes), queries, ((1,), (1,)))
     for row in range(rows):
-        mark = marks[:, row].reshape(tokens, tokens)
+        mark = dot(jnp.where(line == first_line + row, 1.0, 0.0).astype(BF), held)
         for head in range(head_count):
             span = slice(head * tokens, (head + 1) * tokens)
             score = s_ref[row, :, span] * scaling + (bias_ref[:, span] + mark)
@@ -124,71 +162,84 @@
 
 
 def column_moves(me, dy_refs, edge_refs, move_ref, cols):
+    frames, high, _, channels = move_ref.shape
+    channels = channels // 3
+    parts = len(dy_refs)
+    shape = (frames // parts, high, cols, channels)
     blocks = []
     for ref, edge_ref in zip(dy_refs, edge_refs):
+        block = unpack(ref, shape[0] * high * cols, channels).reshape(shape)
         edge = edge_ref[...]
-        first = jnp.where(me == 0, edge, ref[:, :1])
-        last = jnp.where(me == len(dy_refs) - 1, edge, ref[:, -1:])
-        blocks.append(jnp.concatenate([first, ref[:, 1:-1], last], axis=1))
+        first = jnp.where(me == 0, edge, block[:, :1])
+        last = jnp.where(me == parts - 1, edge, block[:, -1:])
+        blocks.append(jnp.concatenate([first, block[:, 1:-1], last], axis=1))
     whole = jnp.concatenate(blocks, axis=0)
     wide = merge_rows(whole).astype(F32)
     count = wide.shape[0]
     col = lax.broadcasted_iota(jnp.int32, wide.shape, 0) % cols
     left = jnp.where(col == cols - 1, 0.0, pltpu.roll(wide, count - 1, 0))
     right = jnp.where(col == 0, 0.0, pltpu.roll(wide, 1, 0))
-    move_ref[0] = left.astype(BF).reshape(whole.shape)
-    move_ref[1] = whole
-    move_ref[2] = right.astype(BF).reshape(whole.shape)
-
-
-def tap_of(moves, row_step, col_step, rows):
-    return merge_rows(moves[col_step + 1, :, 1 - row_step : 1 - row_step + rows])
-
-
-def write_blocks(total_ref, keep_ref, send_ref, place_ref, split, turn=False):
-    if split is None:
-        keep_ref[...] = total_ref[...].astype(BF)
-        return
-    frame_count, height_count, dp_count, size = split
-    for step in range(height_count):
-        for far in range(frame_count):
-            owner = (place_ref[0] ^ far) if frame_count > 1 else 0
-            owner = (owner * height_count + (place_ref[1] ^ step)) * dp_count
-            for ref, side in ((keep_ref, place_ref[2]), (send_ref, 1 - place_ref[2])):
-                first = pl.multiple_of((owner + side) * size, 8)
-                block = total_ref[pl.ds(first, size), :]
-                if turn:
-                    ref[step] = block.T.astype(BF)
-                else:
-                    ref[step, far] = block.astype(BF)
+    for place, moved in enumerate((left.astype(BF).reshape(whole.shape), whole)):
+        move_ref[:, :, :, place * channels : (place + 1) * channels] = moved
+    move_ref[:, :, :, 2 * channels :] = right.astype(BF).reshape(whole.shape)
+
+
+def rows_of(moves, row_step, rows):
+    return merge_rows(moves[:, 1 - row_step : 1 - row_step + rows])
+
+
+def place_block(both_ref, place_ref, split, block, value):
+    frame_count, height_count, dp_count, _ = split
+    step = (block // dp_count % height_count) ^ place_ref[1]
+    side = (block % dp_count) ^ place_ref[2]
+    if frame_count > 1:
+        far = (block // (dp_count * height_count)) ^ place_ref[0]
+        both_ref[side, step, far] = value
+    else:
+        both_ref[side, step] = value
 
 
 def conv_grad_kernel(parts, grad_scale, split, *refs):
     place_ref = refs[0]
     dy_refs = refs[1 : 1 + parts]
     edge_refs = refs[1 + parts : 1 + 2 * parts]
-    a_ref, keep_ref, send_ref, move_ref, total_ref = refs[1 + 2 * parts :]
+    a_ref, both_ref, send_ref, move_ref, total_ref = refs[1 + 2 * parts :]
     _, rows, cols, channels = a_ref.shape
     column_moves(place_ref[0], dy_refs, edge_refs, move_ref, cols)
     act = merge_rows(a_ref[...]).T
-    for tap in range(9):
-        moved = tap_of(move_ref, tap // 3 - 1, tap % 3 - 1, rows)
-        total_ref[tap * channels : (tap + 1) * channels, :] = dot(act, moved) * grad_scale
-    write_blocks(total_ref, keep_ref, send_ref, place_ref, split, turn=True)
+    block = 0
+    for line in range(3):
+        terms = dot(act, rows_of(move_ref, line - 1, rows)) * grad_scale
+        for place in range(3):
+            first = (3 * line + place) * channels
+            total_ref[first : first + channels, :] = terms[:, place * channels : (place + 1) * channels]
+        if split is not None:
+            size = split[3]
+            while (block + 1) * size <= 3 * (line + 1) * channels:
+                value = total_ref[block * size : (block + 1) * size, :].astype(BF).T
+                place_block(both_ref, place_ref, split, block, value)
+                block += 1
+    if split is None:
+        both_ref[...] = total_ref[...].astype(BF)
+    else:
+        send_ref[...] = both_ref[1]
 
 
 def upstream_kernel(channels, grad_scale, *refs):
     moves, y_ref, o_ref, w_ref, conv_ref, g_ref, do_ref, mix_ref = refs
     rows = g_ref.shape[1]
     delta = None
-    for tap in range(9):
-        moved = tap_of(moves, tap // 3 - 1, tap % 3 - 1, rows)
-        term = dot(moved, conv_ref[:, tap * channels : (tap + 1) * channels])
+    for line in range(3):
+        taps = [
+            conv_ref[:, tap * channels : (tap + 1) * channels]
+            for tap in range(3 * line, 3 * line + 3)
+        ]
+        term = dot(rows_of(moves, line - 1, rows), jnp.concatenate(taps, axis=0))
         delta = term if delta is None else delta + term
     value = merge_rows(y_ref[...]).astype(F32)
     sig = sigmoid(value)
     slope = sig * (1.0 + value * (1.0 - sig))
-    dy = tap_of(moves, 0, 0, rows).astype(F32)
+    dy = merge_rows(moves[:, 1 : 1 + rows, :, channels : 2 * channels]).astype(F32)
     upstream = (dy + slope * delta).astype(BF)
     g_ref[...] = upstream.reshape(g_ref.shape)
     back = dot(upstream, w_ref[:, 3 * channels :]).astype(BF)
@@ -198,10 +249,9 @@
 
 def backward_kernel(parts, channels, head_size, grad_scale, split, *refs):
     place_ref = refs[0]
-    x_refs = refs[1 : 1 + parts]
-    (g_ref, do_ref, q_ref, k_ref, v_ref, p_ref, mix_ref, w_ref) = refs[1 + parts : 9 + parts]
-    out_refs = refs[9 + parts : 9 + 2 * parts]
-    keep_ref, send_ref, dq_ref, dk_ref, dv_ref, dp_ref, ds_ref, total_ref = refs[9 + 2 * parts :]
+    (x_ref, g_ref, do_ref, q_ref, k_ref, v_ref, p_ref, mix_ref, w_ref) = refs[1:10]
+    out_refs = refs[10 : 10 + parts]
+    both_ref, send_ref, dq_ref, dk_ref, dv_ref, dp_ref, ds_ref = refs[10 + parts :]
     frames, rows, cols, _ = q_ref.shape
     tokens = frames * cols
     scaling = head_size ** (-0.5)
@@ -239,23 +289,34 @@
     grads = (merge_rows(g_ref[...]).astype(F32) + d_inputs.astype(BF).astype(F32)).astype(BF)
     share = grads.shape[0] // parts
     for step, ref in enumerate(out_refs):
-        ref[...] = grads[step * share : (step + 1) * share].reshape(ref.shape)
-    latents = jnp.concatenate([merge_rows(ref[...])[:, :channels] for ref in x_refs], axis=0)
-    turned = latents.T
-    for place, ref in enumerate((dq_ref, dk_ref, dv_ref)):
-        block = slice(place * channels, (place + 1) * channels)
-        total_ref[block, :] = dot(turned, merge_rows(ref[...])) * grad_scale
-    total_ref[3 * channels :, :] = mix_ref[...]
-    write_blocks(total_ref, keep_ref, send_ref, place_ref, split)
+        pack(ref, grads[step * share : (step + 1) * share])
+    turned = merge_rows(x_ref[...]).T
+    for place, ref in enumerate((dq_ref, dk_ref, dv_ref, mix_ref)):
+        if ref is mix_ref:
+            total = ref[...]
+        else:
+            total = dot(turned, merge_rows(ref[...])) * grad_scale
+        if split is None:
+            both_ref[place * channels : (place + 1) * channels, :] = total.astype(BF)
+            continue
+        size = split[3]
+        for part in range(channels // size):
+            block = place * (channels // size) + part
+            value = total[part * size : (part + 1) * size].astype(BF)
+            place_block(both_ref, place_ref, split, block, value)
+    if split is not None:
+        send_ref[...] = both_ref[1]
 
 
 def place_kernel(parts, *refs):
     place_ref = refs[0]
     part_refs = refs[1 : 1 + parts]
     out_ref = refs[1 + parts]
-    rows = part_refs[0].shape[1]
+    frames, count, cols, channels = out_ref.shape
+    shape = (frames, count // parts, cols, channels)
     for step, ref in enumerate(part_refs):
-        out_ref[:, pl.ds((place_ref[0] ^ step) * rows, rows)] = ref[...]
+        block = unpack(ref, frames * shape[1] * cols, channels).reshape(shape)
+        out_ref[:, pl.ds((place_ref[0] ^ step) * shape[1], shape[1])] = block
 
 
 def prepare_kernel(parts, *refs):
@@ -263,24 +324,11 @@
     x_refs = refs[4 : 4 + parts]
     dy_refs = refs[4 + parts : 4 + 2 * parts]
     edge_refs = refs[4 + 2 * parts : 4 + 3 * parts]
-    x_ref, mask_ref, sems = refs[4 + 3 * parts :]
-    frames, rows, cols, wide = x_refs[0].shape
-    channels = x_ref.shape[-1]
-    count = x_ref.shape[1]
+    x_ref, mask_ref, dy_ref, sems = refs[4 + 3 * parts :]
+    frames, count, cols, channels = x_ref.shape
+    rows = count // parts
     me = place_ref[0]
-    moves = [(x_hbm, x_ref), (mask_hbm, mask_ref)]
-    for step in range(parts):
-        first = (me ^ step) * rows
-        for source, size, to in (
-            (first, rows, 1),
-            (jnp.maximum(first - 1, 0), 1, 0),
-            (jnp.minimum(first + rows, count - 1), 1, rows + 1),
-        ):
-            moves.append(
-                (dy_hbm.at[:, pl.ds(source, size)], dy_refs[step].at[:, pl.ds(to, size)])
-            )
-        row = jnp.where(me == step, count - 1, 0)
-        moves.append((dy_hbm.at[:, pl.ds(row, 1)], edge_refs[step]))
+    moves = ((x_hbm, x_ref), (mask_hbm, mask_ref), (dy_hbm, dy_ref))
     copies = [
         pltpu.make_async_copy(source, target, sems.at[place])
         for place, (source, target) in enumerate(moves)
@@ -289,18 +337,32 @@
         copy.start()
     for copy in copies[:2]:
         copy.wait()
-    blank = jnp.zeros((1, wide - channels - cols), F32)
+    at = packed_rows(frames * rows * cols, channels)
+    lines = x_refs[0].shape[0] - at
     for step, ref in enumerate(x_refs):
         first = (me ^ step) * rows
-        ref[:, :, :, :channels] = x_ref[:, pl.ds(first, rows)]
-        for frame in range(frames):
-            for row in range(rows):
-                line = mask_ref[frame, pl.ds(first + row, 1), :].astype(F32)
-                spare = jnp.concatenate([line, blank], axis=1)
-                spare = jnp.broadcast_to(spare, (cols, wide - channels))
-                ref[frame, row, :, channels:] = spare.astype(BF)
-    for copy in copies[2:]:
-        copy.wait()
+        pack(ref, merge_rows(x_ref[:, pl.ds(first, rows)]))
+        held = [
+            mask_ref[frame, pl.ds(first + row, 1), :].astype(F32)
+            for frame in range(frames)
+            for row in range(rows)
+        ]
+        if lines > len(held):
+            held.append(jnp.zeros((lines - len(held), cols), F32))
+        held = [jnp.concatenate(held, axis=0), jnp.zeros((lines, LANES - cols), F32)]
+        ref[at:, :] = jnp.concatenate(held, axis=1).astype(BF)
+    copies[2].wait()
+    for step, ref in enumerate(dy_refs):
+        first = (me ^ step) * rows
+        block = [
+            dy_ref[:, pl.ds(jnp.maximum(first - 1, 0), 1)],
+            dy_ref[:, pl.ds(first, rows)],
+            dy_ref[:, pl.ds(jnp.minimum(first + rows, count - 1), 1)],
+        ]
+        pack(ref, merge_rows(jnp.concatenate(block, axis=1)))
+    for step, ref in enumerate(edge_refs):
+        row = jnp.where(me == step, count - 1, 0)
+        ref[...] = dy_ref[:, pl.ds(row, 1)]
 
 
 def bias_kernel(head_count, frame_count, cols, *refs):
@@ -346,7 +408,7 @@
 def pair_sum_kernel(*refs):
     left_ref, right_ref = refs[:2]
     for step, ref in enumerate(refs[2:]):
-        ref[...] = (left_ref[step].astype(F32) + right_ref[step].astype(F32)).astype(BF)
+        ref[...] = (left_ref[0, step].astype(F32) + right_ref[step].astype(F32)).astype(BF)
 
 
 def sum_of(refs):
@@ -354,12 +416,6 @@
     for ref in refs[1:]:
         total = total + ref[...].astype(F32)
     return total
-
-
-def spread_sum_kernel(count, *refs):
-    total = sum_of(refs[:count])
-    for step, ref in enumerate(refs[count:]):
-        ref[...] = total[step].astype(ref.dtype)
 
 
 def scatter_sum_kernel(count, *refs):
@@ -376,18 +432,34 @@
         ref[...] = total_ref[pl.ds(first, share), :].astype(BF)
 
 
-def plain_sum_kernel(*refs):
-    refs[-1][...] = sum_of(refs[:-1]).astype(refs[-1].dtype)
-
-
-def gather_kernel(parts, *refs):
+def join_kernel(parts, terms, *refs):
+    share_refs = refs[:parts]
+    term_refs = refs[parts : parts + terms]
+    share, size = share_refs[0].shape
+    _, rows, channels = term_refs[0].shape
+    mine = sum_of(share_refs).astype(BF)
+    total = sum_of(term_refs)
+    for step, ref in enumerate(refs[parts + terms :]):
+        first = up_to(share, 16)
+        ref[:share, :size] = mine
+        ref[first : first + rows, :channels] = total[step].astype(BF)
+
+
+def last_kernel(parts, *refs):
     place_ref = refs[0]
-    out_ref, total_ref = refs[1 + parts :]
-    share = refs[1].shape[0]
-    for step, ref in enumerate(refs[1 : 1 + parts]):
-        first = pl.multiple_of((place_ref[0] ^ step) * share, 8)
-        total_ref[pl.ds(first, share), :] = ref[...].astype(F32)
-    out_ref[...] = total_ref[: out_ref.shape[0], :]
+    part_refs = refs[1 : 1 + parts]
+    conv_ref, attn_ref, total_ref = refs[1 + parts :]
+    channels, size = conv_ref.shape
+    share = total_ref.shape[0] // parts
+    first = up_to(share, 16)
+    attn = None
+    for step, ref in enumerate(part_refs):
+        at = pl.multiple_of((place_ref[0] ^ step) * share, 8)
+        total_ref[pl.ds(at, share), :] = ref[:share, :size].astype(F32)
+        block = ref[first:, : attn_ref.shape[1]].astype(F32)
+        attn = block if attn is None else attn + block
+    conv_ref[...] = total_ref[:channels, :]
+    attn_ref[...] = attn
 
 
 def call(kernel, outs, args, scratch=(), scalars=False, far=0, flops=0):
@@ -414,7 +486,7 @@
 
 def block_size(total, owners):
     size = total // owners
-    return size if size % 8 == 0 else None
+    return size if size % 8 == 0 and size * owners == total else None
 
 
 def pack_blocks(plain, frame_count, height_count, dp_count, me, high, side):
@@ -455,19 +527,21 @@
 
     x = clip_latents[0]
     dy = out_grad[0]
-    spare = -channels % LANES
-    assert cols <= spare
-    wide = like((frame_count, rows, cols, channels + spare))
+    assert cols <= LANES
+    block = frame_count * rows * cols
+    lines = up_to(frame_count * rows, 16)
+    packed = like((packed_rows(block, channels), LANES))
     blocks = call(
         functools.partial(prepare_kernel, parts),
-        [wide] * parts
-        + [like((frame_count, rows + 2, cols, channels))] * parts
+        [like((packed.shape[0] + lines, LANES))] * parts
+        + [like((packed_rows(block + 2 * frame_count * cols, channels), LANES))] * parts
         + [like((frame_count, 1, cols, channels))] * parts,
         [place, x, box_mask[0], dy],
         scratch=[
             pltpu.VMEM(x.shape, BF),
             pltpu.VMEM(box_mask.shape[1:], jnp.int32),
-            pltpu.SemaphoreType.DMA((2 + 4 * parts,)),
+            pltpu.VMEM(dy.shape, BF),
+            pltpu.SemaphoreType.DMA((3,)),
         ],
         scalars=True,
         far=3,
@@ -495,9 +569,9 @@
 
     half = like((all_frames, rows, cols, channels))
     square = (rows, tokens, head_count * tokens)
-    q, k, v, p, o, y, a = call(
+    x_all, q, k, v, p, o, y, a = call(
         functools.partial(forward_kernel, parts, channels, head_size),
-        [half, half, half, like(square, F32), half, half, half],
+        [half, half, half, half, like(square, F32), half, half, half],
         list(x_parts) + [attn_turned, bias],
         scratch=[pltpu.VMEM(square, F32)],
         flops=8 * pixels * channels * channels,
@@ -512,27 +586,28 @@
             return None, [like((total, channels)), like((8, channels))]
         block = (channels, size) if turn else (frames, size, channels)
         shape = like((height_count,) + block)
-        return (frames, height_count, dp_count, size), [shape, shape]
-
-    def over_height(keep, send):
+        both = like((dp_count, height_count) + block)
+        return (frames, height_count, dp_count, size), [both, shape]
+
+    def over_height(both, send):
         got = lax.ppermute(send, "dp", [(0, 1), (1, 0)])
-        both = call(pair_sum_kernel, [like(keep.shape[1:])] * height_count, [keep, got])
-        return trades(both, "height")
+        terms = call(pair_sum_kernel, [like(both.shape[2:])] * height_count, [both, got])
+        return trades(terms, "height")
 
     taps = conv_weights.shape[0]
     split, outs = block_outs(taps, 1, turn=True)
-    keep, send, moves = call(
+    both, send, moves = call(
         functools.partial(conv_grad_kernel, parts, grad_scale, split),
-        outs + [like((3, all_frames, rows + 2, cols, channels))],
+        outs + [like((all_frames, rows + 2, cols, 3 * channels))],
         [place] + dy_parts + edges + [a],
         scratch=[pltpu.VMEM((taps, channels), F32)],
         scalars=True,
         flops=2 * pixels * taps * channels,
     )
     if split is None:
-        keep, send = pack_blocks(keep, 1, height_count, dp_count, 0, high, side)
-        keep, send = jnp.swapaxes(keep[:, 0], 1, 2), jnp.swapaxes(send[:, 0], 1, 2)
-    conv_terms = over_height(keep, send)
+        both, send = pack_blocks(both, 1, height_count, dp_count, 0, high, side)
+        both, send = jnp.swapaxes(both[None, :, 0], 2, 3), jnp.swapaxes(send[:, 0], 1, 2)
+    conv_terms = over_height(both, send)
 
     g, do, mix = call(
         functools.partial(upstream_kernel, channels, grad_scale),
@@ -541,32 +616,23 @@
         flops=2 * pixels * taps * channels,
     )
     split, outs = block_outs(4 * channels, parts)
-    piece = like((frame_count, rows, cols, channels))
     result = call(
         functools.partial(backward_kernel, parts, channels, head_size, grad_scale, split),
-        [piece] * parts + outs,
-        [place] + list(x_parts) + [g, do, q, k, v, p, mix, attn_turned],
+        [packed] * parts + outs,
+        [place, x_all, g, do, q, k, v, p, mix, attn_turned],
         scratch=[pltpu.VMEM(half.shape, BF)] * 3
-        + [pltpu.VMEM(square, F32), pltpu.VMEM(square, BF)]
-        + [pltpu.VMEM((4 * channels, channels), F32)],
+        + [pltpu.VMEM(square, F32), pltpu.VMEM(square, BF)],
         scalars=True,
         flops=2 * pixels * taps * channels,
     )
     grad_parts = [result[0]]
     for step in range(1, parts):
         grad_parts.append(trade(result[step], "frame", step))
-    keep, send = result[parts:]
+    both, send = result[parts:]
     if split is None:
-        keep, send = pack_blocks(keep, parts, height_count, dp_count, me, high, side)
-    attn_terms = over_height(keep, send)
-    shares = call(
-        functools.partial(spread_sum_kernel, height_count),
-        [like(keep.shape[2:])] * parts,
-        attn_terms,
-    )
-    shares = trades(shares, "frame")
-    grad_attn = call(plain_sum_kernel, [like(keep.shape[2:], F32)], shares)[0]
-
+        both, send = pack_blocks(both, parts, height_count, dp_count, me, high, side)
+        both = both[None]
+    attn_terms = over_height(both, send)
     size = conv_terms[0].shape[1]
     share = -(-channels // (parts * 8)) * 8
     shares = call(
@@ -577,22 +643,28 @@
         scalars=True,
     )
     shares = trades(shares, "frame")
-    mine = call(plain_sum_kernel, [like((share, size))], shares)[0]
-    shares = trades([mine] * parts, "frame")
-    grad_conv = call(
-        functools.partial(gather_kernel, parts),
-        [like((channels, size), F32)],
-        [place] + shares,
+    rows_out = send.shape[2]
+    joint = like((up_to(share, 16) + rows_out, max(size, channels)))
+    joined = call(
+        functools.partial(join_kernel, parts, height_count),
+        [joint] * parts,
+        shares + attn_terms,
+    )
+    joined = trades(joined, "frame")
+    grad_conv, grad_attn = call(
+        functools.partial(last_kernel, parts),
+        [like((channels, size), F32), like((rows_out, channels), F32)],
+        [place] + joined,
         scratch=[pltpu.VMEM((parts * share, size), F32)],
         scalars=True,
-    )[0].T
+    )
     grad_input = call(
         functools.partial(place_kernel, parts),
         [like((frame_count, row_count, cols, channels))],
         [place] + grad_parts,
         scalars=True,
     )[0]
-    return (grad_input.reshape(clip_latents.shape), grad_attn, grad_conv)
+    return (grad_input.reshape(clip_latents.shape), grad_attn, grad_conv.T)
 
 
 def solution(mesh):

time: 93.2 us -> 85.8 us (0.921)
  waiting for transfers between devices: 23.5 us -> 20.3 us
  starting transfers between devices: 48.1 us -> 45.5 us
  Pallas kernels: 20.5 us -> 18.9 us
    ppermute x24 -> x21, waiting for transfers between devices: 23.5 us -> 20.3 us  [trade(): lax.ppermute(value, axis, [(i, peer(i, step, count)) for i in range(count)])]
    ppermute x24 -> x21, starting transfers between devices: 42.1 us -> 39.5 us  [trade(): lax.ppermute(value, axis, [(i, peer(i, step, count)) for i in range(count)])]
    pallas_call x14 -> x12, Pallas kernels: 20.5 us -> 18.9 us  [call(): pl.pallas_call(kernel, out_shape=outs, in_specs=specs, out_specs=[vmem] *...]
  transfers between devices with their start and end apart: 30 -> 27, of which waited for: 8 -> 7; matrix products, arithmetic and copies ran while one was open for 0% -> 0% of each run, Pallas kernels for 15% -> 15%
where the time goes in v1:
time: 85.8 us; the launch traced here: 85.6 us
  starting transfers between devices  45.5 us (53%)
  waiting for transfers between devices  20.3 us (24%)
  Pallas kernels  18.9 us (22%)
    ppermute x21, starting transfers between devices, trade(): lax.ppermute(value, axis, [(i, peer(i, step, count)) for i in range(count)])  39.5 us
    ppermute x21, waiting for transfers between devices, trade(): lax.ppermute(value, axis, [(i, peer(i, step, count)) for i in range(count)])  20.3 us
    pallas_call x12, Pallas kernels, call(): pl.pallas_call(kernel, out_shape=outs, in_specs=specs, out_specs=[vmem] *...  18.9 us
    ppermute x4, starting transfers between devices, whole_body(): lax.ppermute(blocks[2 * parts + step], ('frame', 'height'), pairs)  5.37 us
  transfers between devices with their start and end apart: 27, of which 7 were waited for; matrix products, arithmetic and copies ran while one was open for 0% of the time, Pallas kernels for 15%

profile of v1, /device:TPU:0, one launch (start us, length us, event | category | flops | bytes accessed | tf_op | source)
XLA Modules:
  0.0 85.6 jit_solution(2122407149830261713)
XLA Ops:
  0.6 0.1 pad_add_fusion.refs_0_
  0.7 1.8 %shard_map.85 = (bf16[336,128]{1,0:T(8,128)(2,1)S(1)}, bf16[336,128]{1,0:T(8,128)(2,1)S(1)}, bf16[336,128]{1,0:T(8,128)(2,1)S(1)}, bf16[336,128]{1,0:T(8,128)(2,...) custom-call(s32[3]{0:T(128)S(1)} %pad_add_fusion.refs_0_, ...), custom_call_target="tpu_custom_call" | custom-call | bytes 1574924 | tf_op jit(solution)/shard_map/pallas_call | solution.py:476
  2.6 3.1 %collective-permute-start = (bf16[336,128]{1,0:T(8,128)(2,1)S(1)}, bf16[336,128]{1,0:T(8,128)(2,1)S(1)}, u32[]{:S(2)}, u32[]{:S(2)}) collective-permute-start(bf16[336,128]{1,0:T(8,128)(2,1)S(1)} %get-tuple-element.56), channel_id=1, source_target_pairs={{0,8},{8,0},{16,24},{24,16},{1,9},{9,1},{17,25},{25,17},{2,10},{10... | collective-permute-start | bytes 258056 | tf_op jit(solution)/shard_map/ppermute | solution.py:33
  5.7 3.4 %collective-permute-start.6 = (bf16[2,1,16,320]{3,2,1,0:T(8,128)(2,1)S(1)}, bf16[2,1,16,320]{3,2,1,0:T(8,128)(2,1)S(1)}, u32[]{:S(2)}, u32[]{:S(2)}) collective-permute-start(bf16[2,1,16,320]{3,2,1,0:T(8,128)(2,1)S(1)} %get-tuple-element.66), channel_id=1, source_target_pairs={{0,2},{26,24},{2,4},{28,26},{4,6},{30,28},{1,3},{27,25},{3,5},{29,... | collective-permute-start | bytes 61448 | tf_op jit(solution)/shard_map/ppermute | solution.py:559
  9.1 0.7 collective-permute-start.7
  9.7 0.1 collective-permute-start.1
  9.8 6.5 %collective-permute-start.2 = (bf16[336,128]{1,0:T(8,128)(2,1)S(1)}, bf16[336,128]{1,0:T(8,128)(2,1)S(1)}, u32[]{:S(2)}, u32[]{:S(2)}) collective-permute-start(bf16[336,128]{1,0:T(8,128)(2,1)S(1)} %get-tuple-element.58), channel_id=1, source_target_pairs={{0,24},{8,16},{16,8},{24,0},{1,25},{9,17},{17,9},{25,1},{2,26},{10... | collective-permute-start | bytes 258056 | tf_op jit(solution)/shard_map/ppermute | solution.py:33
  16.4 0.0 collective-permute-done.7.refs_6_
  16.4 0.6 collective-permute-start.4
  16.9 3.8 %collective-permute-start.5 = (bf16[480,128]{1,0:T(8,128)(2,1)S(1)}, bf16[480,128]{1,0:T(8,128)(2,1)S(1)}, u32[]{:S(2)}, u32[]{:S(2)}) collective-permute-start(bf16[480,128]{1,0:T(8,128)(2,1)S(1)} %get-tuple-element.65), channel_id=1, source_target_pairs={{0,24},{8,16},{16,8},{24,0},{1,25},{9,17},{17,9},{25,1},{2,26},{10... | collective-permute-start | bytes 368648 | tf_op jit(solution)/shard_map/ppermute | solution.py:33
  20.8 2.3 %shard_map.86 = (f32[128,640]{1,0:T(8,128)S(1)}, bf16[320,1280]{1,0:T(8,128)(2,1)S(1)}) custom-call(s32[3]{0:T(128)S(1)} %pad_add_fusion.refs_0_, f32[5,8,8]{2,1,0:T(8,128)} %refs_1_.1, bf16[320,1280]{1,0:T(8,128)(2,1)} %bitcast.11), custom_call_target="tpu_custom_call" | custom-call | bytes 1967372 | tf_op jit(solution)/shard_map/pallas_call | solution.py:476
  23.1 0.7 collective-permute-start.8
  23.8 0.0 collective-permute-done.2.refs_3_
  23.8 0.7 collective-permute-start.9
  24.4 2.4 %shard_map.87 = (bf16[8,4,16,320]{3,2,1,0:T(8,128)(2,1)S(1)}, bf16[8,4,16,320]{3,2,1,0:T(8,128)(2,1)S(1)}, bf16[8,4,16,320]{3,2,1,0:T(8,128)(2,1)S(1)}, bf16[8,4...) custom-call(bf16[336,128]{1,0:T(8,128)(2,1)S(1)} %get-tuple-element., ...), custom_call_target="tpu_custom_call" | custom-call | flops 419430400 | bytes 5095424 | tf_op jit(solution)/shard_map/pallas_call | solution.py:476
  26.9 0.0 copy-start
  26.9 2.7 %collective-permute-done.4.refs_3_ = bf16[480,128]{1,0:T(8,128)(2,1)S(1)} collective-permute-done((bf16[480,128]{1,0:T(8,128)(2,1)S(1)}, bf16[480,128]{1,0:T(8,128)(2,1)S(1)}, u32[]{:S(2)}, u32[]{:S(2)}) %collective-permute-start.4) | collective-permute-done | bytes 122912 | tf_op jit(solution)/shard_map/ppermute | solution.py:33
  29.6 2.6 %shard_map.88 = (bf16[2,4,320,360]{3,2,1,0:T(8,128)(2,1)S(1)}, bf16[4,320,360]{2,1,0:T(8,128)(2,1)S(1)}, bf16[8,6,16,960]{3,2,1,0:T(8,128)(2,1)S(1)}) custom-call(s32[3]{0:T(128)S(1)} %pad_add_fusion.refs_0_, bf16[480,128]{1,0:T(8,128)(2,1)S(1)} %get-tuple-element.62.refs_1_, bf16[480,128]{1,0:T(8,128)(2,1)S(1)} %collective-permute-done.3.refs_2_, ...), custom_call_target="tpu_custom_call" | custom-call | flops 943718400 | bytes 5140492 | tf_op jit(solution)/shard_map/pallas_call | solution.py:476
  32.3 0.1 collective-permute-start.13
  32.3 2.7 %shard_map.89 = (bf16[8,4,16,320]{3,2,1,0:T(8,128)(2,1)S(1)}, bf16[8,4,16,320]{3,2,1,0:T(8,128)(2,1)S(1)}, f32[320,320]{1,0:T(8,128)S(1)}) custom-call(bf16[8,6,16,960]{3,2,1,0:T(8,128)(2,1)S(1)} %get-tuple-element.71.refs_0_, bf16[8,4,16,320]{3,2,1,0:T(8,128)(2,1)S(1)} %get-tuple-element.72.refs_1_, bf16[8,4,16,320]{3,2,1,0:T(8,128)(2,1)S(1)} %get-tuple-element.73.refs_2_, ...), custom_call_target="tpu_custom_call" | custom-call | flops 943718400 | bytes 5857280 | tf_op jit(solution)/shard_map/pallas_call | solution.py:476
  35.0 3.1 %shard_map.90 = (bf16[320,128]{1,0:T(8,128)(2,1)S(1)}, bf16[320,128]{1,0:T(8,128)(2,1)S(1)}, bf16[320,128]{1,0:T(8,128)(2,1)S(1)}, bf16[320,128]{1,0:T(8,128)(2,...) custom-call(s32[3]{0:T(128)S(1)} %pad_add_fusion.refs_0_, ...), custom_call_target="tpu_custom_call" | custom-call | flops 943718400 | bytes 6062092 | tf_op jit(solution)/shard_map/pallas_call | solution.py:476
  38.1 0.6 collective-permute-start.20
  38.7 0.2 shard_map.92
  38.9 4.8 %collective-permute-start.14 = (bf16[320,360]{1,0:T(8,128)(2,1)S(1)}, bf16[320,360]{1,0:T(8,128)(2,1)S(1)}, u32[]{:S(2)}, u32[]{:S(2)}) collective-permute-start(bf16[320,360]{1,0:T(8,128)(2,1)S(1)} %get-tuple-element.88), channel_id=1, source_target_pairs={{0,2},{2,0},{4,6},{6,4},{1,3},{3,1},{5,7},{7,5},{8,10},{10,8},{12,... | collective-permute-start | bytes 691208 | tf_op jit(solution)/shard_map/ppermute | solution.py:33
  43.7 1.5 %collective-permute-start.15 = (bf16[320,360]{1,0:T(8,128)(2,1)S(1)}, bf16[320,360]{1,0:T(8,128)(2,1)S(1)}, u32[]{:S(2)}, u32[]{:S(2)}) collective-permute-start(bf16[320,360]{1,0:T(8,128)(2,1)S(1)} %get-tuple-element.89), channel_id=1, source_target_pairs={{0,4},{2,6},{4,0},{6,2},{1,5},{3,7},{5,1},{7,3},{8,12},{10,14},{12... | collective-permute-start | bytes 691208 | tf_op jit(solution)/shard_map/ppermute | solution.py:33
  45.2 1.0 %collective-permute-start.16 = (bf16[320,360]{1,0:T(8,128)(2,1)S(1)}, bf16[320,360]{1,0:T(8,128)(2,1)S(1)}, u32[]{:S(2)}, u32[]{:S(2)}) collective-permute-start(bf16[320,360]{1,0:T(8,128)(2,1)S(1)} %get-tuple-element.90), channel_id=1, source_target_pairs={{0,6},{2,4},{4,2},{6,0},{1,7},{3,5},{5,3},{7,1},{8,14},{10,12},{12... | collective-permute-start | bytes 691208 | tf_op jit(solution)/shard_map/ppermute | solution.py:33
  46.2 0.1 shard_map.94
  46.3 1.1 %collective-permute-start.21 = (bf16[4,40,320]{2,1,0:T(8,128)(2,1)S(1)}, bf16[4,40,320]{2,1,0:T(8,128)(2,1)S(1)}, u32[]{:S(2)}, u32[]{:S(2)}) collective-permute-start(bf16[4,40,320]{2,1,0:T(8,128)(2,1)S(1)} %get-tuple-element.98), channel_id=1, source_target_pairs={{0,2},{2,0},{4,6},{6,4},{1,3},{3,1},{5,7},{7,5},{8,10},{10,8},{12,... | collective-permute-start | bytes 307208 | tf_op jit(solution)/shard_map/ppermute | solution.py:33
  47.4 1.5 %collective-permute-start.22 = (bf16[4,40,320]{2,1,0:T(8,128)(2,1)S(1)}, bf16[4,40,320]{2,1,0:T(8,128)(2,1)S(1)}, u32[]{:S(2)}, u32[]{:S(2)}) collective-permute-start(bf16[4,40,320]{2,1,0:T(8,128)(2,1)S(1)} %get-tuple-element.99), channel_id=1, source_target_pairs={{0,4},{2,6},{4,0},{6,2},{1,5},{3,7},{5,1},{7,3},{8,12},{10,14},{12... | collective-permute-start | bytes 307208 | tf_op jit(solution)/shard_map/ppermute | solution.py:33
  48.9 1.6 %collective-permute-done.14.refs_2_ = bf16[320,360]{1,0:T(8,128)(2,1)S(1)} collective-permute-done((bf16[320,360]{1,0:T(8,128)(2,1)S(1)}, bf16[320,360]{1,0:T(8,128)(2,1)S(1)}, u32[]{:S(2)}, u32[]{:S(2)}) %collective-permute-start.14) | collective-permute-done | bytes 230432 | tf_op jit(solution)/shard_map/ppermute | solution.py:33
  50.5 3.0 %collective-permute-start.23 = (bf16[4,40,320]{2,1,0:T(8,128)(2,1)S(1)}, bf16[4,40,320]{2,1,0:T(8,128)(2,1)S(1)}, u32[]{:S(2)}, u32[]{:S(2)}) collective-permute-start(bf16[4,40,320]{2,1,0:T(8,128)(2,1)S(1)} %get-tuple-element.100), channel_id=1, source_target_pairs={{0,6},{2,4},{4,2},{6,0},{1,7},{3,5},{5,3},{7,1},{8,14},{10,12},{12... | collective-permute-start | bytes 307208 | tf_op jit(solution)/shard_map/ppermute | solution.py:33
  53.4 3.8 %collective-permute-done.15.refs_3_ = bf16[320,360]{1,0:T(8,128)(2,1)S(1)} collective-permute-done((bf16[320,360]{1,0:T(8,128)(2,1)S(1)}, bf16[320,360]{1,0:T(8,128)(2,1)S(1)}, u32[]{:S(2)}, u32[]{:S(2)}) %collective-permute-start.15) | collective-permute-done | bytes 230432 | tf_op jit(solution)/shard_map/ppermute | solution.py:33
  57.2 0.9 %collective-permute-start.10 = (bf16[320,128]{1,0:T(8,128)(2,1)S(1)}, bf16[320,128]{1,0:T(8,128)(2,1)S(1)}, u32[]{:S(2)}, u32[]{:S(2)}) collective-permute-start(bf16[320,128]{1,0:T(8,128)(2,1)S(1)} %get-tuple-element.82), channel_id=1, source_target_pairs={{0,8},{8,0},{16,24},{24,16},{1,9},{9,1},{17,25},{25,17},{2,10},{10... | collective-permute-start | bytes 245768 | tf_op jit(solution)/shard_map/ppermute | solution.py:33
  58.2 0.1 collective-permute-done.16.refs_4_
  58.3 0.7 shard_map.93
  59.0 1.1 %collective-permute-start.17 = (bf16[80,360]{1,0:T(8,128)(2,1)S(1)}, bf16[80,360]{1,0:T(8,128)(2,1)S(1)}, u32[]{:S(2)}, u32[]{:S(2)}) collective-permute-start(bf16[80,360]{1,0:T(8,128)(2,1)S(1)} %get-tuple-element.92), channel_id=1, source_target_pairs={{0,8},{8,0},{16,24},{24,16},{1,9},{9,1},{17,25},{25,17},{2,10},{10... | collective-permute-start | bytes 172808 | tf_op jit(solution)/shard_map/ppermute | solution.py:33
  60.1 2.4 %collective-permute-start.18 = (bf16[80,360]{1,0:T(8,128)(2,1)S(1)}, bf16[80,360]{1,0:T(8,128)(2,1)S(1)}, u32[]{:S(2)}, u32[]{:S(2)}) collective-permute-start(bf16[80,360]{1,0:T(8,128)(2,1)S(1)} %get-tuple-element.93), channel_id=1, source_target_pairs={{0,16},{8,24},{16,0},{24,8},{1,17},{9,25},{17,1},{25,9},{2,18},{10... | collective-permute-start | bytes 172808 | tf_op jit(solution)/shard_map/ppermute | solution.py:33
  62.5 2.0 %collective-permute-start.19 = (bf16[80,360]{1,0:T(8,128)(2,1)S(1)}, bf16[80,360]{1,0:T(8,128)(2,1)S(1)}, u32[]{:S(2)}, u32[]{:S(2)}) collective-permute-start(bf16[80,360]{1,0:T(8,128)(2,1)S(1)} %get-tuple-element.94), channel_id=1, source_target_pairs={{0,24},{8,16},{16,8},{24,0},{1,25},{9,17},{17,9},{25,1},{2,26},{10... | collective-permute-start | bytes 172808 | tf_op jit(solution)/shard_map/ppermute | solution.py:33
  64.5 0.7 collective-permute-done.18.refs_2_
  65.2 4.0 %collective-permute-done.19.refs_3_ = bf16[80,360]{1,0:T(8,128)(2,1)S(1)} collective-permute-done((bf16[80,360]{1,0:T(8,128)(2,1)S(1)}, bf16[80,360]{1,0:T(8,128)(2,1)S(1)}, u32[]{:S(2)}, u32[]{:S(2)}) %collective-permute-start.19) | collective-permute-done | bytes 57632 | tf_op jit(solution)/shard_map/ppermute | solution.py:33
  69.2 0.1 shard_map.95
  69.3 0.2 collective-permute-start.24
  69.4 2.2 %collective-permute-start.25 = (bf16[120,360]{1,0:T(8,128)(2,1)S(1)}, bf16[120,360]{1,0:T(8,128)(2,1)S(1)}, u32[]{:S(2)}, u32[]{:S(2)}) collective-permute-start(bf16[120,360]{1,0:T(8,128)(2,1)S(1)} %get-tuple-element.103), channel_id=1, source_target_pairs={{0,16},{8,24},{16,0},{24,8},{1,17},{9,25},{17,1},{25,9},{2,18},{10... | collective-permute-start | bytes 259208 | tf_op jit(solution)/shard_map/ppermute | solution.py:33
  71.7 2.1 %collective-permute-start.26 = (bf16[120,360]{1,0:T(8,128)(2,1)S(1)}, bf16[120,360]{1,0:T(8,128)(2,1)S(1)}, u32[]{:S(2)}, u32[]{:S(2)}) collective-permute-start(bf16[120,360]{1,0:T(8,128)(2,1)S(1)} %get-tuple-element.104), channel_id=1, source_target_pairs={{0,24},{8,16},{16,8},{24,0},{1,25},{9,17},{17,9},{25,1},{2,26},{10... | collective-permute-start | bytes 259208 | tf_op jit(solution)/shard_map/ppermute | solution.py:33
  73.7 1.7 %collective-permute-start.12 = (bf16[320,128]{1,0:T(8,128)(2,1)S(1)}, bf16[320,128]{1,0:T(8,128)(2,1)S(1)}, u32[]{:S(2)}, u32[]{:S(2)}) collective-permute-start(bf16[320,128]{1,0:T(8,128)(2,1)S(1)} %get-tuple-element.84), channel_id=1, source_target_pairs={{0,24},{8,16},{16,8},{24,0},{1,25},{9,17},{17,9},{25,1},{2,26},{10... | collective-permute-start | bytes 245768 | tf_op jit(solution)/shard_map/ppermute | solution.py:33
  75.5 7.4 %collective-permute-done.11.refs_3_ = bf16[320,128]{1,0:T(8,128)(2,1)S(1)} collective-permute-done((bf16[320,128]{1,0:T(8,128)(2,1)S(1)}, bf16[320,128]{1,0:T(8,128)(2,1)S(1)}, u32[]{:S(2)}, u32[]{:S(2)}) %collective-permute-start.11) | collective-permute-done | bytes 81952 | tf_op jit(solution)/shard_map/ppermute | solution.py:33
  82.8 1.4 %shard_map.91 = bf16[2,16,16,320]{3,2,1,0:T(8,128)(2,1)} custom-call(s32[3]{0:T(128)S(1)} %pad_add_fusion.refs_0_, bf16[320,128]{1,0:T(8,128)(2,1)S(1)} %get-tuple-element.81.refs_1_, bf16[320,128]{1,0:T(8,128)(2,1)S(1)} %collective-permute-done.10.refs_2_, bf16[320,128]{1,0:T(8,128)(2,1)S(1)} %collective-permute-done.11.refs_3_, ...), custom_call_target="tpu_custom_call" | custom-call | bytes 655372 | tf_op jit(solution)/shard_map/pallas_call | solution.py:476
  84.3 1.4 %shard_map.96 = (f32[320,360]{1,0:T(8,128)}, f32[40,320]{1,0:T(8,128)}) custom-call(s32[3]{0:T(128)S(1)} %pad_add_fusion.refs_0_, bf16[120,360]{1,0:T(8,128)(2,1)S(1)} %get-tuple-element.101.refs_1_, bf16[120,360]{1,0:T(8,128)(2,1)S(1)} %collective-permute-done.24.refs_2_, bf16[120,360]{1,0:T(8,128)(2,1)S(1)} %collective-permute-done.25.refs_3_, ...), custom_call_target="tpu_custom_call" | custom-call | bytes 857612 | tf_op jit(solution)/shard_map/pallas_call | solution.py:476
  (21 shorter events, 0.1 us)
Async XLA Ops:
  2.6 14.4 %collective-permute-start = (bf16[336,128]{1,0:T(8,128)(2,1)S(1)}, bf16[336,128]{1,0:T(8,128)(2,1)S(1)}, u32[]{:S(2)}, u32[]{:S(2)}) collective-permute-start(bf16[336,128]{1,0:T(8,128)(2,1)S(1)} %get-tuple-element.56), channel_id=1, source_target_pairs={{0,8},{8,0},{16,24},{24,16},{1,9},{9,1},{17,25},{25,17},{2,10},{10... | collective-permute-start | bytes 258056 | tf_op jit(solution)/shard_map/ppermute | solution.py:33
  5.7 10.7 %collective-permute-start.6 = (bf16[2,1,16,320]{3,2,1,0:T(8,128)(2,1)S(1)}, bf16[2,1,16,320]{3,2,1,0:T(8,128)(2,1)S(1)}, u32[]{:S(2)}, u32[]{:S(2)}) collective-permute-start(bf16[2,1,16,320]{3,2,1,0:T(8,128)(2,1)S(1)} %get-tuple-element.66), channel_id=1, source_target_pairs={{0,2},{26,24},{2,4},{28,26},{4,6},{30,28},{1,3},{27,25},{3,5},{29,... | collective-permute-start | bytes 61448 | tf_op jit(solution)/shard_map/ppermute | solution.py:559
  9.1 7.3 %collective-permute-start.7 = (bf16[2,1,16,320]{3,2,1,0:T(8,128)(2,1)S(1)}, bf16[2,1,16,320]{3,2,1,0:T(8,128)(2,1)S(1)}, u32[]{:S(2)}, u32[]{:S(2)}) collective-permute-start(bf16[2,1,16,320]{3,2,1,0:T(8,128)(2,1)S(1)} %get-tuple-element.67), channel_id=1, source_target_pairs={{8,2},{18,24},{10,4},{20,26},{12,6},{22,28},{9,3},{19,25},{11,5},{... | collective-permute-start | bytes 61448 | tf_op jit(solution)/shard_map/ppermute | solution.py:559
  9.7 13.3 %collective-permute-start.1 = (bf16[336,128]{1,0:T(8,128)(2,1)S(1)}, bf16[336,128]{1,0:T(8,128)(2,1)S(1)}, u32[]{:S(2)}, u32[]{:S(2)}) collective-permute-start(bf16[336,128]{1,0:T(8,128)(2,1)S(1)} %get-tuple-element.57), channel_id=1, source_target_pairs={{0,16},{8,24},{16,0},{24,8},{1,17},{9,25},{17,1},{25,9},{2,18},{10... | collective-permute-start | bytes 258056 | tf_op jit(solution)/shard_map/ppermute | solution.py:33
  9.8 13.9 %collective-permute-start.2 = (bf16[336,128]{1,0:T(8,128)(2,1)S(1)}, bf16[336,128]{1,0:T(8,128)(2,1)S(1)}, u32[]{:S(2)}, u32[]{:S(2)}) collective-permute-start(bf16[336,128]{1,0:T(8,128)(2,1)S(1)} %get-tuple-element.58), channel_id=1, source_target_pairs={{0,24},{8,16},{16,8},{24,0},{1,25},{9,17},{17,9},{25,1},{2,26},{10... | collective-permute-start | bytes 258056 | tf_op jit(solution)/shard_map/ppermute | solution.py:33
  16.4 10.5 %collective-permute-start.3 = (bf16[480,128]{1,0:T(8,128)(2,1)S(1)}, bf16[480,128]{1,0:T(8,128)(2,1)S(1)}, u32[]{:S(2)}, u32[]{:S(2)}) collective-permute-start(bf16[480,128]{1,0:T(8,128)(2,1)S(1)} %get-tuple-element.63), channel_id=1, source_target_pairs={{0,8},{8,0},{16,24},{24,16},{1,9},{9,1},{17,25},{25,17},{2,10},{10... | collective-permute-start | bytes 368648 | tf_op jit(solution)/shard_map/ppermute | solution.py:33
  16.4 13.2 %collective-permute-start.4 = (bf16[480,128]{1,0:T(8,128)(2,1)S(1)}, bf16[480,128]{1,0:T(8,128)(2,1)S(1)}, u32[]{:S(2)}, u32[]{:S(2)}) collective-permute-start(bf16[480,128]{1,0:T(8,128)(2,1)S(1)} %get-tuple-element.64), channel_id=1, source_target_pairs={{0,16},{8,24},{16,0},{24,8},{1,17},{9,25},{17,1},{25,9},{2,18},{10... | collective-permute-start | bytes 368648 | tf_op jit(solution)/shard_map/ppermute | solution.py:33
  16.9 12.7 %collective-permute-start.5 = (bf16[480,128]{1,0:T(8,128)(2,1)S(1)}, bf16[480,128]{1,0:T(8,128)(2,1)S(1)}, u32[]{:S(2)}, u32[]{:S(2)}) collective-permute-start(bf16[480,128]{1,0:T(8,128)(2,1)S(1)} %get-tuple-element.65), channel_id=1, source_target_pairs={{0,24},{8,16},{16,8},{24,0},{1,25},{9,17},{17,9},{25,1},{2,26},{10... | collective-permute-start | bytes 368648 | tf_op jit(solution)/shard_map/ppermute | solution.py:33
  23.1 3.8 %collective-permute-start.8 = (bf16[2,1,16,320]{3,2,1,0:T(8,128)(2,1)S(1)}, bf16[2,1,16,320]{3,2,1,0:T(8,128)(2,1)S(1)}, u32[]{:S(2)}, u32[]{:S(2)}) collective-permute-start(bf16[2,1,16,320]{3,2,1,0:T(8,128)(2,1)S(1)} %get-tuple-element.68), channel_id=1, source_target_pairs={{16,2},{10,24},{18,4},{12,26},{20,6},{14,28},{17,3},{11,25},{19,5}... | collective-permute-start | bytes 61448 | tf_op jit(solution)/shard_map/ppermute | solution.py:559
  23.8 3.1 %collective-permute-start.9 = (bf16[2,1,16,320]{3,2,1,0:T(8,128)(2,1)S(1)}, bf16[2,1,16,320]{3,2,1,0:T(8,128)(2,1)S(1)}, u32[]{:S(2)}, u32[]{:S(2)}) collective-permute-start(bf16[2,1,16,320]{3,2,1,0:T(8,128)(2,1)S(1)} %get-tuple-element.69), channel_id=1, source_target_pairs={{24,2},{2,24},{26,4},{4,26},{28,6},{6,28},{25,3},{3,25},{27,5},{5,... | collective-permute-start | bytes 61448 | tf_op jit(solution)/shard_map/ppermute | solution.py:559
  26.9 5.5 %copy-start = (bf16[2880,320]{0,1:T(8,128)(2,1)S(1)}, bf16[2880,320]{0,1:T(8,128)(2,1)}, u32[]{:S(2)}) copy-start(bf16[2880,320]{0,1:T(8,128)(2,1)} %param.10) | copy-start | bytes 5529604
  32.3 6.4 %collective-permute-start.13 = (bf16[4,320,360]{2,1,0:T(8,128)(2,1)S(1)}, bf16[4,320,360]{2,1,0:T(8,128)(2,1)S(1)}, u32[]{:S(2)}, u32[]{:S(2)}) collective-permute-start(bf16[4,320,360]{2,1,0:T(8,128)(2,1)S(1)} %get-tuple-element.86), channel_id=1, source_target_pairs={{0,1},{1,0},{2,3},{3,2},{4,5},{5,4},{6,7},{7,6},{8,9},{9,8},{10,11... | collective-permute-start | bytes 2764808 | tf_op jit(solution)/shard_map/ppermute | solution.py:593
  38.1 8.1 %collective-permute-start.20 = (bf16[4,4,40,320]{3,2,1,0:T(8,128)(2,1)S(1)}, bf16[4,4,40,320]{3,2,1,0:T(8,128)(2,1)S(1)}, u32[]{:S(2)}, u32[]{:S(2)}) collective-permute-start(bf16[4,4,40,320]{3,2,1,0:T(8,128)(2,1)S(1)} %get-tuple-element.96), channel_id=1, source_target_pairs={{0,1},{1,0},{2,3},{3,2},{4,5},{5,4},{6,7},{7,6},{8,9},{9,8},{10,11... | collective-permute-start | bytes 1228808 | tf_op jit(solution)/shard_map/ppermute | solution.py:593
  38.9 11.6 %collective-permute-start.14 = (bf16[320,360]{1,0:T(8,128)(2,1)S(1)}, bf16[320,360]{1,0:T(8,128)(2,1)S(1)}, u32[]{:S(2)}, u32[]{:S(2)}) collective-permute-start(bf16[320,360]{1,0:T(8,128)(2,1)S(1)} %get-tuple-element.88), channel_id=1, source_target_pairs={{0,2},{2,0},{4,6},{6,4},{1,3},{3,1},{5,7},{7,5},{8,10},{10,8},{12,... | collective-permute-start | bytes 691208 | tf_op jit(solution)/shard_map/ppermute | solution.py:33
  43.7 13.6 %collective-permute-start.15 = (bf16[320,360]{1,0:T(8,128)(2,1)S(1)}, bf16[320,360]{1,0:T(8,128)(2,1)S(1)}, u32[]{:S(2)}, u32[]{:S(2)}) collective-permute-start(bf16[320,360]{1,0:T(8,128)(2,1)S(1)} %get-tuple-element.89), channel_id=1, source_target_pairs={{0,4},{2,6},{4,0},{6,2},{1,5},{3,7},{5,1},{7,3},{8,12},{10,14},{12... | collective-permute-start | bytes 691208 | tf_op jit(solution)/shard_map/ppermute | solution.py:33
  45.2 13.1 %collective-permute-start.16 = (bf16[320,360]{1,0:T(8,128)(2,1)S(1)}, bf16[320,360]{1,0:T(8,128)(2,1)S(1)}, u32[]{:S(2)}, u32[]{:S(2)}) collective-permute-start(bf16[320,360]{1,0:T(8,128)(2,1)S(1)} %get-tuple-element.90), channel_id=1, source_target_pairs={{0,6},{2,4},{4,2},{6,0},{1,7},{3,5},{5,3},{7,1},{8,14},{10,12},{12... | collective-permute-start | bytes 691208 | tf_op jit(solution)/shard_map/ppermute | solution.py:33
  46.3 13.8 %collective-permute-start.21 = (bf16[4,40,320]{2,1,0:T(8,128)(2,1)S(1)}, bf16[4,40,320]{2,1,0:T(8,128)(2,1)S(1)}, u32[]{:S(2)}, u32[]{:S(2)}) collective-permute-start(bf16[4,40,320]{2,1,0:T(8,128)(2,1)S(1)} %get-tuple-element.98), channel_id=1, source_target_pairs={{0,2},{2,0},{4,6},{6,4},{1,3},{3,1},{5,7},{7,5},{8,10},{10,8},{12,... | collective-permute-start | bytes 307208 | tf_op jit(solution)/shard_map/ppermute | solution.py:33
  47.4 15.1 %collective-permute-start.22 = (bf16[4,40,320]{2,1,0:T(8,128)(2,1)S(1)}, bf16[4,40,320]{2,1,0:T(8,128)(2,1)S(1)}, u32[]{:S(2)}, u32[]{:S(2)}) collective-permute-start(bf16[4,40,320]{2,1,0:T(8,128)(2,1)S(1)} %get-tuple-element.99), channel_id=1, source_target_pairs={{0,4},{2,6},{4,0},{6,2},{1,5},{3,7},{5,1},{7,3},{8,12},{10,14},{12... | collective-permute-start | bytes 307208 | tf_op jit(solution)/shard_map/ppermute | solution.py:33
  50.5 14.1 %collective-permute-start.23 = (bf16[4,40,320]{2,1,0:T(8,128)(2,1)S(1)}, bf16[4,40,320]{2,1,0:T(8,128)(2,1)S(1)}, u32[]{:S(2)}, u32[]{:S(2)}) collective-permute-start(bf16[4,40,320]{2,1,0:T(8,128)(2,1)S(1)} %get-tuple-element.100), channel_id=1, source_target_pairs={{0,6},{2,4},{4,2},{6,0},{1,7},{3,5},{5,3},{7,1},{8,14},{10,12},{12... | collective-permute-start | bytes 307208 | tf_op jit(solution)/shard_map/ppermute | solution.py:33
  57.2 16.5 %collective-permute-start.10 = (bf16[320,128]{1,0:T(8,128)(2,1)S(1)}, bf16[320,128]{1,0:T(8,128)(2,1)S(1)}, u32[]{:S(2)}, u32[]{:S(2)}) collective-permute-start(bf16[320,128]{1,0:T(8,128)(2,1)S(1)} %get-tuple-element.82), channel_id=1, source_target_pairs={{0,8},{8,0},{16,24},{24,16},{1,9},{9,1},{17,25},{25,17},{2,10},{10... | collective-permute-start | bytes 245768 | tf_op jit(solution)/shard_map/ppermute | solution.py:33
  59.0 5.5 %collective-permute-start.17 = (bf16[80,360]{1,0:T(8,128)(2,1)S(1)}, bf16[80,360]{1,0:T(8,128)(2,1)S(1)}, u32[]{:S(2)}, u32[]{:S(2)}) collective-permute-start(bf16[80,360]{1,0:T(8,128)(2,1)S(1)} %get-tuple-element.92), channel_id=1, source_target_pairs={{0,8},{8,0},{16,24},{24,16},{1,9},{9,1},{17,25},{25,17},{2,10},{10... | collective-permute-start | bytes 172808 | tf_op jit(solution)/shard_map/ppermute | solution.py:33
  60.1 5.1 %collective-permute-start.18 = (bf16[80,360]{1,0:T(8,128)(2,1)S(1)}, bf16[80,360]{1,0:T(8,128)(2,1)S(1)}, u32[]{:S(2)}, u32[]{:S(2)}) collective-permute-start(bf16[80,360]{1,0:T(8,128)(2,1)S(1)} %get-tuple-element.93), channel_id=1, source_target_pairs={{0,16},{8,24},{16,0},{24,8},{1,17},{9,25},{17,1},{25,9},{2,18},{10... | collective-permute-start | bytes 172808 | tf_op jit(solution)/shard_map/ppermute | solution.py:33
  62.5 6.7 %collective-permute-start.19 = (bf16[80,360]{1,0:T(8,128)(2,1)S(1)}, bf16[80,360]{1,0:T(8,128)(2,1)S(1)}, u32[]{:S(2)}, u32[]{:S(2)}) collective-permute-start(bf16[80,360]{1,0:T(8,128)(2,1)S(1)} %get-tuple-element.94), channel_id=1, source_target_pairs={{0,24},{8,16},{16,8},{24,0},{1,25},{9,17},{17,9},{25,1},{2,26},{10... | collective-permute-start | bytes 172808 | tf_op jit(solution)/shard_map/ppermute | solution.py:33
  69.3 15.0 %collective-permute-start.24 = (bf16[120,360]{1,0:T(8,128)(2,1)S(1)}, bf16[120,360]{1,0:T(8,128)(2,1)S(1)}, u32[]{:S(2)}, u32[]{:S(2)}) collective-permute-start(bf16[120,360]{1,0:T(8,128)(2,1)S(1)} %get-tuple-element.102), channel_id=1, source_target_pairs={{0,8},{8,0},{16,24},{24,16},{1,9},{9,1},{17,25},{25,17},{2,10},{10... | collective-permute-start | bytes 259208 | tf_op jit(solution)/shard_map/ppermute | solution.py:33
  69.4 14.8 %collective-permute-start.25 = (bf16[120,360]{1,0:T(8,128)(2,1)S(1)}, bf16[120,360]{1,0:T(8,128)(2,1)S(1)}, u32[]{:S(2)}, u32[]{:S(2)}) collective-permute-start(bf16[120,360]{1,0:T(8,128)(2,1)S(1)} %get-tuple-element.103), channel_id=1, source_target_pairs={{0,16},{8,24},{16,0},{24,8},{1,17},{9,25},{17,1},{25,9},{2,18},{10... | collective-permute-start | bytes 259208 | tf_op jit(solution)/shard_map/ppermute | solution.py:33
  71.7 12.6 %collective-permute-start.26 = (bf16[120,360]{1,0:T(8,128)(2,1)S(1)}, bf16[120,360]{1,0:T(8,128)(2,1)S(1)}, u32[]{:S(2)}, u32[]{:S(2)}) collective-permute-start(bf16[120,360]{1,0:T(8,128)(2,1)S(1)} %get-tuple-element.104), channel_id=1, source_target_pairs={{0,24},{8,16},{16,8},{24,0},{1,25},{9,17},{17,9},{25,1},{2,26},{10... | collective-permute-start | bytes 259208 | tf_op jit(solution)/shard_map/ppermute | solution.py:33
  73.7 9.1 %collective-permute-start.11 = (bf16[320,128]{1,0:T(8,128)(2,1)S(1)}, bf16[320,128]{1,0:T(8,128)(2,1)S(1)}, u32[]{:S(2)}, u32[]{:S(2)}) collective-permute-start(bf16[320,128]{1,0:T(8,128)(2,1)S(1)} %get-tuple-element.83), channel_id=1, source_target_pairs={{0,16},{8,24},{16,0},{24,8},{1,17},{9,25},{17,1},{25,9},{2,18},{10... | collective-permute-start | bytes 245768 | tf_op jit(solution)/shard_map/ppermute | solution.py:33
  73.7 9.1 %collective-permute-start.12 = (bf16[320,128]{1,0:T(8,128)(2,1)S(1)}, bf16[320,128]{1,0:T(8,128)(2,1)S(1)}, u32[]{:S(2)}, u32[]{:S(2)}) collective-permute-start(bf16[320,128]{1,0:T(8,128)(2,1)S(1)} %get-tuple-element.84), channel_id=1, source_target_pairs={{0,24},{8,16},{16,8},{24,0},{1,25},{9,17},{17,9},{25,1},{2,26},{10... | collective-permute-start | bytes 245768 | tf_op jit(solution)/shard_map/ppermute | solution.py:33

commit v2 on v1

--- a/solution.py
+++ b/solution.py
@@ -161,18 +161,12 @@
     a_ref[...] = (value * sigmoid(value)).astype(BF).reshape(a_ref.shape)
 
 
-def column_moves(me, dy_refs, edge_refs, move_ref, cols):
+def column_moves(dy_refs, move_ref, cols):
     frames, high, _, channels = move_ref.shape
     channels = channels // 3
     parts = len(dy_refs)
     shape = (frames // parts, high, cols, channels)
-    blocks = []
-    for ref, edge_ref in zip(dy_refs, edge_refs):
-        block = unpack(ref, shape[0] * high * cols, channels).reshape(shape)
-        edge = edge_ref[...]
-        first = jnp.where(me == 0, edge, block[:, :1])
-        last = jnp.where(me == parts - 1, edge, block[:, -1:])
-        blocks.append(jnp.concatenate([first, block[:, 1:-1], last], axis=1))
+    blocks = [unpack(ref, shape[0] * high * cols, channels).reshape(shape) for ref in dy_refs]
     whole = jnp.concatenate(blocks, axis=0)
     wide = merge_rows(whole).astype(F32)
     count = wide.shape[0]
@@ -202,10 +196,9 @@
 def conv_grad_kernel(parts, grad_scale, split, *refs):
     place_ref = refs[0]
     dy_refs = refs[1 : 1 + parts]
-    edge_refs = refs[1 + parts : 1 + 2 * parts]
-    a_ref, both_ref, send_ref, move_ref, total_ref = refs[1 + 2 * parts :]
+    a_ref, both_ref, send_ref, move_ref, total_ref = refs[1 + parts :]
     _, rows, cols, channels = a_ref.shape
-    column_moves(place_ref[0], dy_refs, edge_refs, move_ref, cols)
+    column_moves(dy_refs, move_ref, cols)
     act = merge_rows(a_ref[...]).T
     block = 0
     for line in range(3):
@@ -322,9 +315,7 @@
 def prepare_kernel(parts, *refs):
     place_ref, x_hbm, mask_hbm, dy_hbm = refs[:4]
     x_refs = refs[4 : 4 + parts]
-    dy_refs = refs[4 + parts : 4 + 2 * parts]
-    edge_refs = refs[4 + 2 * parts : 4 + 3 * parts]
-    x_ref, mask_ref, dy_ref, sems = refs[4 + 3 * parts :]
+    dy_ref, one_ref, two_ref, x_ref, mask_ref, sems = refs[4 + parts :]
     frames, count, cols, channels = x_ref.shape
     rows = count // parts
     me = place_ref[0]
@@ -352,17 +343,28 @@
         held = [jnp.concatenate(held, axis=0), jnp.zeros((lines, LANES - cols), F32)]
         ref[at:, :] = jnp.concatenate(held, axis=1).astype(BF)
     copies[2].wait()
-    for step, ref in enumerate(dy_refs):
-        first = (me ^ step) * rows
+    odd = place_ref[1] % 2
+    one_ref[...] = dy_ref[:, pl.ds((1 - odd) * (count - 1), 1)]
+    two_ref[...] = dy_ref[:, pl.ds(odd * (count - 1), 1)]
+
+
+def halo_kernel(parts, *refs):
+    place_ref, dy_ref, one_ref, two_ref = refs[:4]
+    count = dy_ref.shape[1]
+    rows = count // parts
+    odd = place_ref[1] % 2 == 1
+    low = jnp.where(odd, one_ref[...], two_ref[...])
+    top = jnp.where(odd, two_ref[...], one_ref[...])
+    for step, ref in enumerate(refs[4:]):
+        first = (place_ref[0] ^ step) * rows
+        above = dy_ref[:, pl.ds(jnp.maximum(first - 1, 0), 1)]
+        below = dy_ref[:, pl.ds(jnp.minimum(first + rows, count - 1), 1)]
         block = [
-            dy_ref[:, pl.ds(jnp.maximum(first - 1, 0), 1)],
+            jnp.where(first == 0, low, above),
             dy_ref[:, pl.ds(first, rows)],
-            dy_ref[:, pl.ds(jnp.minimum(first + rows, count - 1), 1)],
+            jnp.where(first + rows == count, top, below),
         ]
         pack(ref, merge_rows(jnp.concatenate(block, axis=1)))
-    for step, ref in enumerate(edge_refs):
-        row = jnp.where(me == step, count - 1, 0)
-        ref[...] = dy_ref[:, pl.ds(row, 1)]
 
 
 def bias_kernel(head_count, frame_count, cols, *refs):
@@ -420,13 +422,18 @@
 
 def scatter_sum_kernel(count, *refs):
     place_ref = refs[0]
+    term_refs = refs[1 : 1 + count]
     out_refs = refs[1 + count : -1]
     total_ref = refs[-1]
     share = out_refs[0].shape[0]
-    total = sum_of(refs[1 : 1 + count])
-    if total.shape[0] < total_ref.shape[0]:
-        total_ref[...] = jnp.zeros(total_ref.shape, F32)
-    total_ref[: total.shape[0], :] = total
+    rows = term_refs[0].shape[0]
+    if share * len(out_refs) == rows and share % 16 == 0:
+        for step, ref in enumerate(out_refs):
+            first = pl.multiple_of((place_ref[0] ^ step) * share, 16)
+            ref[...] = sum_of([term.at[pl.ds(first, share)] for term in term_refs]).astype(BF)
+        return
+    total_ref[...] = jnp.zeros(total_ref.shape, F32)
+    total_ref[:rows, :] = sum_of(term_refs)
     for step, ref in enumerate(out_refs):
         first = pl.multiple_of((place_ref[0] ^ step) * share, 8)
         ref[...] = total_ref[pl.ds(first, share), :].astype(BF)
@@ -515,15 +522,16 @@
     side = lax.axis_index("dp")
     rows = row_count // parts
     assert clips == 1 and dp_count == 2 and rows * parts == row_count
-    assert is_pow2(parts) and is_pow2(height_count)
+    assert is_pow2(parts) and is_pow2(height_count) and height_count > 1
     tokens = all_frames * cols
     pixels = tokens * rows
     place = jnp.stack([me, high, side]).astype(jnp.int32)
 
     def trades(values, axis):
-        return [values[0]] + [
-            trade(values[step], axis, step) for step in range(1, lax.axis_size(axis))
-        ]
+        result = [values[0]]
+        for step in range(1, lax.axis_size(axis)):
+            result.append(trade(values[step], axis, step))
+        return result
 
     x = clip_latents[0]
     dy = out_grad[0]
@@ -534,29 +542,29 @@
     blocks = call(
         functools.partial(prepare_kernel, parts),
         [like((packed.shape[0] + lines, LANES))] * parts
-        + [like((packed_rows(block + 2 * frame_count * cols, channels), LANES))] * parts
-        + [like((frame_count, 1, cols, channels))] * parts,
+        + [like(dy.shape)]
+        + [like((frame_count, 1, cols, channels))] * 2,
         [place, x, box_mask[0], dy],
         scratch=[
             pltpu.VMEM(x.shape, BF),
             pltpu.VMEM(box_mask.shape[1:], jnp.int32),
-            pltpu.VMEM(dy.shape, BF),
             pltpu.SemaphoreType.DMA((3,)),
         ],
         scalars=True,
         far=3,
     )
     x_parts = trades(blocks[:parts], "frame")
-
-    last = parts - 1
-    dy_parts = trades(blocks[parts : 2 * parts], "frame")
-    edges = []
-    for step in range(parts):
-        pairs = []
-        for i in range(height_count - 1):
-            pairs.append((step * height_count + i, i + 1))
-            pairs.append(((last ^ step) * height_count + i + 1, last * height_count + i))
-        edges.append(lax.ppermute(blocks[2 * parts + step], ("frame", "height"), pairs))
+    dy, one, two = blocks[parts:]
+    swaps = [(i, i + 1) for i in range(1, height_count - 1, 2)]
+    two = lax.ppermute(two, "height", swaps + [(j, i) for i, j in swaps])
+    one = trade(one, "height", 1)
+    blocks = call(
+        functools.partial(halo_kernel, parts),
+        [like((packed_rows(block + 2 * frame_count * cols, channels), LANES))] * parts,
+        [place, dy, one, two],
+        scalars=True,
+    )
+    dy_parts = trades(blocks, "frame")
 
     bias, attn_turned = call(
         functools.partial(bias_kernel, head_count, frame_count, cols),
@@ -599,7 +607,7 @@
     both, send, moves = call(
         functools.partial(conv_grad_kernel, parts, grad_scale, split),
         outs + [like((all_frames, rows + 2, cols, 3 * channels))],
-        [place] + dy_parts + edges + [a],
+        [place] + dy_parts + [a],
         scratch=[pltpu.VMEM((taps, channels), F32)],
         scalars=True,
         flops=2 * pixels * taps * channels,
@@ -625,9 +633,7 @@
         scalars=True,
         flops=2 * pixels * taps * channels,
     )
-    grad_parts = [result[0]]
-    for step in range(1, parts):
-        grad_parts.append(trade(result[step], "frame", step))
+    grad_parts = trades(result[:parts], "frame")
     both, send = result[parts:]
     if split is None:
         both, send = pack_blocks(both, parts, height_count, dp_count, me, high, side)

time: 85.8 us -> 84 us (0.979)
  starting transfers between devices: 45.5 us -> 32.1 us
  waiting for transfers between devices: 20.3 us -> 31.5 us
    ppermute x21 -> x22, waiting for transfers between devices: 20.3 us -> 31.4 us  [trade(): lax.ppermute(value, axis, [(i, peer(i, step, count)) for i in range(count)])]
    ppermute x21 -> x22, starting transfers between devices: 39.5 us -> 30.8 us  [trade(): lax.ppermute(value, axis, [(i, peer(i, step, count)) for i in range(count)])]
    ppermute x4 -> x1, starting transfers between devices: 5.37 us -> 0.65 us  [whole_body(): two = lax.ppermute(two, 'height', swaps + [(j, i) for i, j in swaps])]
    pallas_call x12 -> x13, Pallas kernels: 18.9 us -> 19.4 us  [call(): pl.pallas_call(kernel, out_shape=outs, in_specs=specs, out_specs=[vmem] *...]
  transfers between devices with their start and end apart: 27 -> 25, of which waited for: 7 -> 7; matrix products, arithmetic and copies ran while one was open for 0% -> 0% of each run, Pallas kernels for 15% -> 16%
where the time goes in v2:
time: 84 us; the launch traced here: 83.9 us
  starting transfers between devices  32.1 us (38%)
  waiting for transfers between devices  31.5 us (38%)
  Pallas kernels  19.4 us (23%)
    ppermute x22, waiting for transfers between devices, trade(): lax.ppermute(value, axis, [(i, peer(i, step, count)) for i in range(count)])  31.4 us
    ppermute x22, starting transfers between devices, trade(): lax.ppermute(value, axis, [(i, peer(i, step, count)) for i in range(count)])  30.8 us
    pallas_call x13, Pallas kernels, call(): pl.pallas_call(kernel, out_shape=outs, in_specs=specs, out_specs=[vmem] *...  19.4 us
  transfers between devices with their start and end apart: 25, of which 7 were waited for; matrix products, arithmetic and copies ran while one was open for 0% of the time, Pallas kernels for 16%

profile of v2, /device:TPU:0, one launch (start us, length us, event | category | flops | bytes accessed | tf_op | source)
XLA Modules:
  0.0 83.9 jit_solution(14181893369348766186)
XLA Ops:
  0.6 0.1 pad_add_fusion.refs_0_
  0.7 1.7 %shard_map.85 = (bf16[336,128]{1,0:T(8,128)(2,1)S(1)}, bf16[336,128]{1,0:T(8,128)(2,1)S(1)}, bf16[336,128]{1,0:T(8,128)(2,1)S(1)}, bf16[336,128]{1,0:T(8,128)(2,...) custom-call(s32[3]{0:T(128)S(1)} %pad_add_fusion.refs_0_, ...), custom_call_target="tpu_custom_call" | custom-call | bytes 1370124 | tf_op jit(solution)/shard_map/pallas_call | solution.py:483
  2.4 3.1 %collective-permute-start = (bf16[336,128]{1,0:T(8,128)(2,1)S(1)}, bf16[336,128]{1,0:T(8,128)(2,1)S(1)}, u32[]{:S(2)}, u32[]{:S(2)}) collective-permute-start(bf16[336,128]{1,0:T(8,128)(2,1)S(1)} %get-tuple-element.55), channel_id=1, source_target_pairs={{0,8},{8,0},{16,24},{24,16},{1,9},{9,1},{17,25},{25,17},{2,10},{10... | collective-permute-start | bytes 258056 | tf_op jit(solution)/shard_map/ppermute | solution.py:33
  5.5 1.5 %collective-permute-start.3 = (bf16[2,1,16,320]{3,2,1,0:T(8,128)(2,1)S(1)}, bf16[2,1,16,320]{3,2,1,0:T(8,128)(2,1)S(1)}, u32[]{:S(2)}, u32[]{:S(2)}) collective-permute-start(bf16[2,1,16,320]{3,2,1,0:T(8,128)(2,1)S(1)} %get-tuple-element.62), channel_id=1, source_target_pairs={{0,2},{2,0},{4,6},{6,4},{1,3},{3,1},{5,7},{7,5},{8,10},{10,8},{12,... | collective-permute-start | bytes 61448 | tf_op jit(solution)/shard_map/ppermute | solution.py:33
  7.0 0.7 collective-permute-start.4
  7.7 2.7 %collective-permute-start.1 = (bf16[336,128]{1,0:T(8,128)(2,1)S(1)}, bf16[336,128]{1,0:T(8,128)(2,1)S(1)}, u32[]{:S(2)}, u32[]{:S(2)}) collective-permute-start(bf16[336,128]{1,0:T(8,128)(2,1)S(1)} %get-tuple-element.56), channel_id=1, source_target_pairs={{0,16},{8,24},{16,0},{24,8},{1,17},{9,25},{17,1},{25,9},{2,18},{10... | collective-permute-start | bytes 258056 | tf_op jit(solution)/shard_map/ppermute | solution.py:33
  10.3 0.2 collective-permute-start.2
  10.6 0.0 collective-permute-done.4.refs_3_
  10.6 0.7 shard_map.88
  11.3 0.7 collective-permute-start.5
  12.0 3.5 %collective-permute-start.6 = (bf16[480,128]{1,0:T(8,128)(2,1)S(1)}, bf16[480,128]{1,0:T(8,128)(2,1)S(1)}, u32[]{:S(2)}, u32[]{:S(2)}) collective-permute-start(bf16[480,128]{1,0:T(8,128)(2,1)S(1)} %get-tuple-element.66), channel_id=1, source_target_pairs={{0,16},{8,24},{16,0},{24,8},{1,17},{9,25},{17,1},{25,9},{2,18},{10... | collective-permute-start | bytes 368648 | tf_op jit(solution)/shard_map/ppermute | solution.py:33
  15.5 0.0 collective-permute-done.refs_1_
  15.5 0.2 collective-permute-start.7
  15.7 2.3 %shard_map.86 = (f32[128,640]{1,0:T(8,128)S(1)}, bf16[320,1280]{1,0:T(8,128)(2,1)S(1)}) custom-call(s32[3]{0:T(128)S(1)} %pad_add_fusion.refs_0_, f32[5,8,8]{2,1,0:T(8,128)} %refs_1_.1, bf16[320,1280]{1,0:T(8,128)(2,1)} %bitcast.11), custom_call_target="tpu_custom_call" | custom-call | bytes 1967372 | tf_op jit(solution)/shard_map/pallas_call | solution.py:483
  18.1 2.4 %shard_map.87 = (bf16[8,4,16,320]{3,2,1,0:T(8,128)(2,1)S(1)}, bf16[8,4,16,320]{3,2,1,0:T(8,128)(2,1)S(1)}, bf16[8,4,16,320]{3,2,1,0:T(8,128)(2,1)S(1)}, bf16[8,4...) custom-call(bf16[336,128]{1,0:T(8,128)(2,1)S(1)} %get-tuple-element., ...), custom_call_target="tpu_custom_call" | custom-call | flops 419430400 | bytes 5095424 | tf_op jit(solution)/shard_map/pallas_call | solution.py:483
  20.5 0.0 copy-start
  20.5 0.0 collective-permute-done.5.refs_2_
  20.5 6.0 %collective-permute-done.6.refs_3_ = bf16[480,128]{1,0:T(8,128)(2,1)S(1)} collective-permute-done((bf16[480,128]{1,0:T(8,128)(2,1)S(1)}, bf16[480,128]{1,0:T(8,128)(2,1)S(1)}, u32[]{:S(2)}, u32[]{:S(2)}) %collective-permute-start.6) | collective-permute-done | bytes 122912 | tf_op jit(solution)/shard_map/ppermute | solution.py:33
  26.6 0.0 collective-permute-done.7.refs_4_
  26.6 2.6 %shard_map.89 = (bf16[2,4,320,360]{3,2,1,0:T(8,128)(2,1)S(1)}, bf16[4,320,360]{2,1,0:T(8,128)(2,1)S(1)}, bf16[8,6,16,960]{3,2,1,0:T(8,128)(2,1)S(1)}) custom-call(s32[3]{0:T(128)S(1)} %pad_add_fusion.refs_0_, bf16[480,128]{1,0:T(8,128)(2,1)S(1)} %get-tuple-element.64.refs_1_, bf16[480,128]{1,0:T(8,128)(2,1)S(1)} %collective-permute-done.5.refs_2_, ...), custom_call_target="tpu_custom_call" | custom-call | flops 943718400 | bytes 5058572 | tf_op jit(solution)/shard_map/pallas_call | solution.py:483
  29.2 0.1 collective-permute-start.11
  29.3 2.7 %shard_map.90 = (bf16[8,4,16,320]{3,2,1,0:T(8,128)(2,1)S(1)}, bf16[8,4,16,320]{3,2,1,0:T(8,128)(2,1)S(1)}, f32[320,320]{1,0:T(8,128)S(1)}) custom-call(bf16[8,6,16,960]{3,2,1,0:T(8,128)(2,1)S(1)} %get-tuple-element.69.refs_0_, bf16[8,4,16,320]{3,2,1,0:T(8,128)(2,1)S(1)} %get-tuple-element.70.refs_1_, bf16[8,4,16,320]{3,2,1,0:T(8,128)(2,1)S(1)} %get-tuple-element.71.refs_2_, ...), custom_call_target="tpu_custom_call" | custom-call | flops 943718400 | bytes 5857280 | tf_op jit(solution)/shard_map/pallas_call | solution.py:483
  32.0 3.1 %shard_map.91 = (bf16[320,128]{1,0:T(8,128)(2,1)S(1)}, bf16[320,128]{1,0:T(8,128)(2,1)S(1)}, bf16[320,128]{1,0:T(8,128)(2,1)S(1)}, bf16[320,128]{1,0:T(8,128)(2,...) custom-call(s32[3]{0:T(128)S(1)} %pad_add_fusion.refs_0_, ...), custom_call_target="tpu_custom_call" | custom-call | flops 943718400 | bytes 6062092 | tf_op jit(solution)/shard_map/pallas_call | solution.py:483
  35.0 0.6 collective-permute-start.18
  35.6 0.2 shard_map.93
  35.8 4.3 %collective-permute-start.12 = (bf16[320,360]{1,0:T(8,128)(2,1)S(1)}, bf16[320,360]{1,0:T(8,128)(2,1)S(1)}, u32[]{:S(2)}, u32[]{:S(2)}) collective-permute-start(bf16[320,360]{1,0:T(8,128)(2,1)S(1)} %get-tuple-element.86), channel_id=1, source_target_pairs={{0,2},{2,0},{4,6},{6,4},{1,3},{3,1},{5,7},{7,5},{8,10},{10,8},{12,... | collective-permute-start | bytes 691208 | tf_op jit(solution)/shard_map/ppermute | solution.py:33
  40.1 1.5 %collective-permute-start.14 = (bf16[320,360]{1,0:T(8,128)(2,1)S(1)}, bf16[320,360]{1,0:T(8,128)(2,1)S(1)}, u32[]{:S(2)}, u32[]{:S(2)}) collective-permute-start(bf16[320,360]{1,0:T(8,128)(2,1)S(1)} %get-tuple-element.88), channel_id=1, source_target_pairs={{0,6},{2,4},{4,2},{6,0},{1,7},{3,5},{5,3},{7,1},{8,14},{10,12},{12... | collective-permute-start | bytes 691208 | tf_op jit(solution)/shard_map/ppermute | solution.py:33
  41.7 0.1 shard_map.95
  41.8 2.0 %collective-permute-start.19 = (bf16[4,40,320]{2,1,0:T(8,128)(2,1)S(1)}, bf16[4,40,320]{2,1,0:T(8,128)(2,1)S(1)}, u32[]{:S(2)}, u32[]{:S(2)}) collective-permute-start(bf16[4,40,320]{2,1,0:T(8,128)(2,1)S(1)} %get-tuple-element.96), channel_id=1, source_target_pairs={{0,2},{2,0},{4,6},{6,4},{1,3},{3,1},{5,7},{7,5},{8,10},{10,8},{12,... | collective-permute-start | bytes 307208 | tf_op jit(solution)/shard_map/ppermute | solution.py:33
  43.8 3.1 %collective-permute-done.12.refs_2_ = bf16[320,360]{1,0:T(8,128)(2,1)S(1)} collective-permute-done((bf16[320,360]{1,0:T(8,128)(2,1)S(1)}, bf16[320,360]{1,0:T(8,128)(2,1)S(1)}, u32[]{:S(2)}, u32[]{:S(2)}) %collective-permute-start.12) | collective-permute-done | bytes 230432 | tf_op jit(solution)/shard_map/ppermute | solution.py:33
  46.9 0.2 collective-permute-start.21
  47.1 9.8 %collective-permute-done.13.refs_3_ = bf16[320,360]{1,0:T(8,128)(2,1)S(1)} collective-permute-done((bf16[320,360]{1,0:T(8,128)(2,1)S(1)}, bf16[320,360]{1,0:T(8,128)(2,1)S(1)}, u32[]{:S(2)}, u32[]{:S(2)}) %collective-permute-start.13) | collective-permute-done | bytes 230432 | tf_op jit(solution)/shard_map/ppermute | solution.py:33
  56.9 0.2 collective-permute-start.8
  57.1 0.7 shard_map.94
  57.8 1.9 %collective-permute-start.15 = (bf16[80,360]{1,0:T(8,128)(2,1)S(1)}, bf16[80,360]{1,0:T(8,128)(2,1)S(1)}, u32[]{:S(2)}, u32[]{:S(2)}) collective-permute-start(bf16[80,360]{1,0:T(8,128)(2,1)S(1)} %get-tuple-element.90), channel_id=1, source_target_pairs={{0,8},{8,0},{16,24},{24,16},{1,9},{9,1},{17,25},{25,17},{2,10},{10... | collective-permute-start | bytes 172808 | tf_op jit(solution)/shard_map/ppermute | solution.py:33
  59.6 1.3 %collective-permute-start.16 = (bf16[80,360]{1,0:T(8,128)(2,1)S(1)}, bf16[80,360]{1,0:T(8,128)(2,1)S(1)}, u32[]{:S(2)}, u32[]{:S(2)}) collective-permute-start(bf16[80,360]{1,0:T(8,128)(2,1)S(1)} %get-tuple-element.91), channel_id=1, source_target_pairs={{0,16},{8,24},{16,0},{24,8},{1,17},{9,25},{17,1},{25,9},{2,18},{10... | collective-permute-start | bytes 172808 | tf_op jit(solution)/shard_map/ppermute | solution.py:33
  60.9 1.3 %collective-permute-start.17 = (bf16[80,360]{1,0:T(8,128)(2,1)S(1)}, bf16[80,360]{1,0:T(8,128)(2,1)S(1)}, u32[]{:S(2)}, u32[]{:S(2)}) collective-permute-start(bf16[80,360]{1,0:T(8,128)(2,1)S(1)} %get-tuple-element.92), channel_id=1, source_target_pairs={{0,24},{8,16},{16,8},{24,0},{1,25},{9,17},{17,9},{25,1},{2,26},{10... | collective-permute-start | bytes 172808 | tf_op jit(solution)/shard_map/ppermute | solution.py:33
  62.2 0.3 collective-permute-done.15.refs_1_
  62.5 2.5 %collective-permute-done.16.refs_2_ = bf16[80,360]{1,0:T(8,128)(2,1)S(1)} collective-permute-done((bf16[80,360]{1,0:T(8,128)(2,1)S(1)}, bf16[80,360]{1,0:T(8,128)(2,1)S(1)}, u32[]{:S(2)}, u32[]{:S(2)}) %collective-permute-start.16) | collective-permute-done | bytes 57632 | tf_op jit(solution)/shard_map/ppermute | solution.py:33
  65.1 2.1 %collective-permute-done.17.refs_3_ = bf16[80,360]{1,0:T(8,128)(2,1)S(1)} collective-permute-done((bf16[80,360]{1,0:T(8,128)(2,1)S(1)}, bf16[80,360]{1,0:T(8,128)(2,1)S(1)}, u32[]{:S(2)}, u32[]{:S(2)}) %collective-permute-start.17) | collective-permute-done | bytes 57632 | tf_op jit(solution)/shard_map/ppermute | solution.py:33
  67.1 0.1 shard_map.96
  67.2 0.1 collective-permute-start.22
  67.3 2.3 %collective-permute-start.23 = (bf16[120,360]{1,0:T(8,128)(2,1)S(1)}, bf16[120,360]{1,0:T(8,128)(2,1)S(1)}, u32[]{:S(2)}, u32[]{:S(2)}) collective-permute-start(bf16[120,360]{1,0:T(8,128)(2,1)S(1)} %get-tuple-element.101), channel_id=1, source_target_pairs={{0,16},{8,24},{16,0},{24,8},{1,17},{9,25},{17,1},{25,9},{2,18},{10... | collective-permute-start | bytes 259208 | tf_op jit(solution)/shard_map/ppermute | solution.py:33
  69.6 2.1 %collective-permute-start.24 = (bf16[120,360]{1,0:T(8,128)(2,1)S(1)}, bf16[120,360]{1,0:T(8,128)(2,1)S(1)}, u32[]{:S(2)}, u32[]{:S(2)}) collective-permute-start(bf16[120,360]{1,0:T(8,128)(2,1)S(1)} %get-tuple-element.102), channel_id=1, source_target_pairs={{0,24},{8,16},{16,8},{24,0},{1,25},{9,17},{17,9},{25,1},{2,26},{10... | collective-permute-start | bytes 259208 | tf_op jit(solution)/shard_map/ppermute | solution.py:33
  71.7 1.8 %collective-permute-start.10 = (bf16[320,128]{1,0:T(8,128)(2,1)S(1)}, bf16[320,128]{1,0:T(8,128)(2,1)S(1)}, u32[]{:S(2)}, u32[]{:S(2)}) collective-permute-start(bf16[320,128]{1,0:T(8,128)(2,1)S(1)} %get-tuple-element.82), channel_id=1, source_target_pairs={{0,24},{8,16},{16,8},{24,0},{1,25},{9,17},{17,9},{25,1},{2,26},{10... | collective-permute-start | bytes 245768 | tf_op jit(solution)/shard_map/ppermute | solution.py:33
  73.5 7.6 %collective-permute-done.9.refs_3_ = bf16[320,128]{1,0:T(8,128)(2,1)S(1)} collective-permute-done((bf16[320,128]{1,0:T(8,128)(2,1)S(1)}, bf16[320,128]{1,0:T(8,128)(2,1)S(1)}, u32[]{:S(2)}, u32[]{:S(2)}) %collective-permute-start.9) | collective-permute-done | bytes 81952 | tf_op jit(solution)/shard_map/ppermute | solution.py:33
  81.1 1.4 %shard_map.92 = bf16[2,16,16,320]{3,2,1,0:T(8,128)(2,1)} custom-call(s32[3]{0:T(128)S(1)} %pad_add_fusion.refs_0_, bf16[320,128]{1,0:T(8,128)(2,1)S(1)} %get-tuple-element.79.refs_1_, bf16[320,128]{1,0:T(8,128)(2,1)S(1)} %collective-permute-done.8.refs_2_, bf16[320,128]{1,0:T(8,128)(2,1)S(1)} %collective-permute-done.9.refs_3_, ...), custom_call_target="tpu_custom_call" | custom-call | bytes 655372 | tf_op jit(solution)/shard_map/pallas_call | solution.py:483
  82.5 1.4 %shard_map.97 = (f32[320,360]{1,0:T(8,128)}, f32[40,320]{1,0:T(8,128)}) custom-call(s32[3]{0:T(128)S(1)} %pad_add_fusion.refs_0_, bf16[120,360]{1,0:T(8,128)(2,1)S(1)} %get-tuple-element.99.refs_1_, bf16[120,360]{1,0:T(8,128)(2,1)S(1)} %collective-permute-done.22.refs_2_, bf16[120,360]{1,0:T(8,128)(2,1)S(1)} %collective-permute-done.23.refs_3_, ...), custom_call_target="tpu_custom_call" | custom-call | bytes 857612 | tf_op jit(solution)/shard_map/pallas_call | solution.py:483
  (18 shorter events, 0.0 us)
Async XLA Ops:
  2.4 13.1 %collective-permute-start = (bf16[336,128]{1,0:T(8,128)(2,1)S(1)}, bf16[336,128]{1,0:T(8,128)(2,1)S(1)}, u32[]{:S(2)}, u32[]{:S(2)}) collective-permute-start(bf16[336,128]{1,0:T(8,128)(2,1)S(1)} %get-tuple-element.55), channel_id=1, source_target_pairs={{0,8},{8,0},{16,24},{24,16},{1,9},{9,1},{17,25},{25,17},{2,10},{10... | collective-permute-start | bytes 258056 | tf_op jit(solution)/shard_map/ppermute | solution.py:33
  5.5 5.0 %collective-permute-start.3 = (bf16[2,1,16,320]{3,2,1,0:T(8,128)(2,1)S(1)}, bf16[2,1,16,320]{3,2,1,0:T(8,128)(2,1)S(1)}, u32[]{:S(2)}, u32[]{:S(2)}) collective-permute-start(bf16[2,1,16,320]{3,2,1,0:T(8,128)(2,1)S(1)} %get-tuple-element.62), channel_id=1, source_target_pairs={{0,2},{2,0},{4,6},{6,4},{1,3},{3,1},{5,7},{7,5},{8,10},{10,8},{12,... | collective-permute-start | bytes 61448 | tf_op jit(solution)/shard_map/ppermute | solution.py:33
  7.0 3.5 %collective-permute-start.4 = (bf16[2,1,16,320]{3,2,1,0:T(8,128)(2,1)S(1)}, bf16[2,1,16,320]{3,2,1,0:T(8,128)(2,1)S(1)}, u32[]{:S(2)}, u32[]{:S(2)}) collective-permute-start(bf16[2,1,16,320]{3,2,1,0:T(8,128)(2,1)S(1)} %get-tuple-element.63), channel_id=1, source_target_pairs={{2,4},{4,2},{3,5},{5,3},{10,12},{12,10},{11,13},{13,11},{18,20},{2... | collective-permute-start | bytes 61448 | tf_op jit(solution)/shard_map/ppermute | solution.py:559
  7.7 10.3 %collective-permute-start.1 = (bf16[336,128]{1,0:T(8,128)(2,1)S(1)}, bf16[336,128]{1,0:T(8,128)(2,1)S(1)}, u32[]{:S(2)}, u32[]{:S(2)}) collective-permute-start(bf16[336,128]{1,0:T(8,128)(2,1)S(1)} %get-tuple-element.56), channel_id=1, source_target_pairs={{0,16},{8,24},{16,0},{24,8},{1,17},{9,25},{17,1},{25,9},{2,18},{10... | collective-permute-start | bytes 258056 | tf_op jit(solution)/shard_map/ppermute | solution.py:33
  10.3 7.7 %collective-permute-start.2 = (bf16[336,128]{1,0:T(8,128)(2,1)S(1)}, bf16[336,128]{1,0:T(8,128)(2,1)S(1)}, u32[]{:S(2)}, u32[]{:S(2)}) collective-permute-start(bf16[336,128]{1,0:T(8,128)(2,1)S(1)} %get-tuple-element.57), channel_id=1, source_target_pairs={{0,24},{8,16},{16,8},{24,0},{1,25},{9,17},{17,9},{25,1},{2,26},{10... | collective-permute-start | bytes 258056 | tf_op jit(solution)/shard_map/ppermute | solution.py:33
  11.3 9.2 %collective-permute-start.5 = (bf16[480,128]{1,0:T(8,128)(2,1)S(1)}, bf16[480,128]{1,0:T(8,128)(2,1)S(1)}, u32[]{:S(2)}, u32[]{:S(2)}) collective-permute-start(bf16[480,128]{1,0:T(8,128)(2,1)S(1)} %get-tuple-element.65), channel_id=1, source_target_pairs={{0,8},{8,0},{16,24},{24,16},{1,9},{9,1},{17,25},{25,17},{2,10},{10... | collective-permute-start | bytes 368648 | tf_op jit(solution)/shard_map/ppermute | solution.py:33
  12.0 14.5 %collective-permute-start.6 = (bf16[480,128]{1,0:T(8,128)(2,1)S(1)}, bf16[480,128]{1,0:T(8,128)(2,1)S(1)}, u32[]{:S(2)}, u32[]{:S(2)}) collective-permute-start(bf16[480,128]{1,0:T(8,128)(2,1)S(1)} %get-tuple-element.66), channel_id=1, source_target_pairs={{0,16},{8,24},{16,0},{24,8},{1,17},{9,25},{17,1},{25,9},{2,18},{10... | collective-permute-start | bytes 368648 | tf_op jit(solution)/shard_map/ppermute | solution.py:33
  15.5 11.1 %collective-permute-start.7 = (bf16[480,128]{1,0:T(8,128)(2,1)S(1)}, bf16[480,128]{1,0:T(8,128)(2,1)S(1)}, u32[]{:S(2)}, u32[]{:S(2)}) collective-permute-start(bf16[480,128]{1,0:T(8,128)(2,1)S(1)} %get-tuple-element.67), channel_id=1, source_target_pairs={{0,24},{8,16},{16,8},{24,0},{1,25},{9,17},{17,9},{25,1},{2,26},{10... | collective-permute-start | bytes 368648 | tf_op jit(solution)/shard_map/ppermute | solution.py:33
  20.5 8.8 %copy-start = (bf16[2880,320]{0,1:T(8,128)(2,1)S(1)}, bf16[2880,320]{0,1:T(8,128)(2,1)}, u32[]{:S(2)}) copy-start(bf16[2880,320]{0,1:T(8,128)(2,1)} %param.10) | copy-start | bytes 5529604
  29.2 6.4 %collective-permute-start.11 = (bf16[4,320,360]{2,1,0:T(8,128)(2,1)S(1)}, bf16[4,320,360]{2,1,0:T(8,128)(2,1)S(1)}, u32[]{:S(2)}, u32[]{:S(2)}) collective-permute-start(bf16[4,320,360]{2,1,0:T(8,128)(2,1)S(1)} %get-tuple-element.84), channel_id=1, source_target_pairs={{0,1},{1,0},{2,3},{3,2},{4,5},{5,4},{6,7},{7,6},{8,9},{9,8},{10,11... | collective-permute-start | bytes 2764808 | tf_op jit(solution)/shard_map/ppermute | solution.py:601
  35.0 6.6 %collective-permute-start.18 = (bf16[4,4,40,320]{3,2,1,0:T(8,128)(2,1)S(1)}, bf16[4,4,40,320]{3,2,1,0:T(8,128)(2,1)S(1)}, u32[]{:S(2)}, u32[]{:S(2)}) collective-permute-start(bf16[4,4,40,320]{3,2,1,0:T(8,128)(2,1)S(1)} %get-tuple-element.94), channel_id=1, source_target_pairs={{0,1},{1,0},{2,3},{3,2},{4,5},{5,4},{6,7},{7,6},{8,9},{9,8},{10,11... | collective-permute-start | bytes 1228808 | tf_op jit(solution)/shard_map/ppermute | solution.py:601
  35.8 11.1 %collective-permute-start.12 = (bf16[320,360]{1,0:T(8,128)(2,1)S(1)}, bf16[320,360]{1,0:T(8,128)(2,1)S(1)}, u32[]{:S(2)}, u32[]{:S(2)}) collective-permute-start(bf16[320,360]{1,0:T(8,128)(2,1)S(1)} %get-tuple-element.86), channel_id=1, source_target_pairs={{0,2},{2,0},{4,6},{6,4},{1,3},{3,1},{5,7},{7,5},{8,10},{10,8},{12,... | collective-permute-start | bytes 691208 | tf_op jit(solution)/shard_map/ppermute | solution.py:33
  40.1 16.7 %collective-permute-start.13 = (bf16[320,360]{1,0:T(8,128)(2,1)S(1)}, bf16[320,360]{1,0:T(8,128)(2,1)S(1)}, u32[]{:S(2)}, u32[]{:S(2)}) collective-permute-start(bf16[320,360]{1,0:T(8,128)(2,1)S(1)} %get-tuple-element.87), channel_id=1, source_target_pairs={{0,4},{2,6},{4,0},{6,2},{1,5},{3,7},{5,1},{7,3},{8,12},{10,14},{12... | collective-permute-start | bytes 691208 | tf_op jit(solution)/shard_map/ppermute | solution.py:33
  40.1 16.9 %collective-permute-start.14 = (bf16[320,360]{1,0:T(8,128)(2,1)S(1)}, bf16[320,360]{1,0:T(8,128)(2,1)S(1)}, u32[]{:S(2)}, u32[]{:S(2)}) collective-permute-start(bf16[320,360]{1,0:T(8,128)(2,1)S(1)} %get-tuple-element.88), channel_id=1, source_target_pairs={{0,6},{2,4},{4,2},{6,0},{1,7},{3,5},{5,3},{7,1},{8,14},{10,12},{12... | collective-permute-start | bytes 691208 | tf_op jit(solution)/shard_map/ppermute | solution.py:33
  41.8 17.8 %collective-permute-start.19 = (bf16[4,40,320]{2,1,0:T(8,128)(2,1)S(1)}, bf16[4,40,320]{2,1,0:T(8,128)(2,1)S(1)}, u32[]{:S(2)}, u32[]{:S(2)}) collective-permute-start(bf16[4,40,320]{2,1,0:T(8,128)(2,1)S(1)} %get-tuple-element.96), channel_id=1, source_target_pairs={{0,2},{2,0},{4,6},{6,4},{1,3},{3,1},{5,7},{7,5},{8,10},{10,8},{12,... | collective-permute-start | bytes 307208 | tf_op jit(solution)/shard_map/ppermute | solution.py:33
  43.8 17.1 %collective-permute-start.20 = (bf16[4,40,320]{2,1,0:T(8,128)(2,1)S(1)}, bf16[4,40,320]{2,1,0:T(8,128)(2,1)S(1)}, u32[]{:S(2)}, u32[]{:S(2)}) collective-permute-start(bf16[4,40,320]{2,1,0:T(8,128)(2,1)S(1)} %get-tuple-element.97), channel_id=1, source_target_pairs={{0,4},{2,6},{4,0},{6,2},{1,5},{3,7},{5,1},{7,3},{8,12},{10,14},{12... | collective-permute-start | bytes 307208 | tf_op jit(solution)/shard_map/ppermute | solution.py:33
  46.9 15.3 %collective-permute-start.21 = (bf16[4,40,320]{2,1,0:T(8,128)(2,1)S(1)}, bf16[4,40,320]{2,1,0:T(8,128)(2,1)S(1)}, u32[]{:S(2)}, u32[]{:S(2)}) collective-permute-start(bf16[4,40,320]{2,1,0:T(8,128)(2,1)S(1)} %get-tuple-element.98), channel_id=1, source_target_pairs={{0,6},{2,4},{4,2},{6,0},{1,7},{3,5},{5,3},{7,1},{8,14},{10,12},{12... | collective-permute-start | bytes 307208 | tf_op jit(solution)/shard_map/ppermute | solution.py:33
  56.9 14.8 %collective-permute-start.8 = (bf16[320,128]{1,0:T(8,128)(2,1)S(1)}, bf16[320,128]{1,0:T(8,128)(2,1)S(1)}, u32[]{:S(2)}, u32[]{:S(2)}) collective-permute-start(bf16[320,128]{1,0:T(8,128)(2,1)S(1)} %get-tuple-element.80), channel_id=1, source_target_pairs={{0,8},{8,0},{16,24},{24,16},{1,9},{9,1},{17,25},{25,17},{2,10},{10... | collective-permute-start | bytes 245768 | tf_op jit(solution)/shard_map/ppermute | solution.py:33
  57.8 4.8 %collective-permute-start.15 = (bf16[80,360]{1,0:T(8,128)(2,1)S(1)}, bf16[80,360]{1,0:T(8,128)(2,1)S(1)}, u32[]{:S(2)}, u32[]{:S(2)}) collective-permute-start(bf16[80,360]{1,0:T(8,128)(2,1)S(1)} %get-tuple-element.90), channel_id=1, source_target_pairs={{0,8},{8,0},{16,24},{24,16},{1,9},{9,1},{17,25},{25,17},{2,10},{10... | collective-permute-start | bytes 172808 | tf_op jit(solution)/shard_map/ppermute | solution.py:33
  59.6 5.4 %collective-permute-start.16 = (bf16[80,360]{1,0:T(8,128)(2,1)S(1)}, bf16[80,360]{1,0:T(8,128)(2,1)S(1)}, u32[]{:S(2)}, u32[]{:S(2)}) collective-permute-start(bf16[80,360]{1,0:T(8,128)(2,1)S(1)} %get-tuple-element.91), channel_id=1, source_target_pairs={{0,16},{8,24},{16,0},{24,8},{1,17},{9,25},{17,1},{25,9},{2,18},{10... | collective-permute-start | bytes 172808 | tf_op jit(solution)/shard_map/ppermute | solution.py:33
  60.9 6.2 %collective-permute-start.17 = (bf16[80,360]{1,0:T(8,128)(2,1)S(1)}, bf16[80,360]{1,0:T(8,128)(2,1)S(1)}, u32[]{:S(2)}, u32[]{:S(2)}) collective-permute-start(bf16[80,360]{1,0:T(8,128)(2,1)S(1)} %get-tuple-element.92), channel_id=1, source_target_pairs={{0,24},{8,16},{16,8},{24,0},{1,25},{9,17},{17,9},{25,1},{2,26},{10... | collective-permute-start | bytes 172808 | tf_op jit(solution)/shard_map/ppermute | solution.py:33
  67.2 15.2 %collective-permute-start.22 = (bf16[120,360]{1,0:T(8,128)(2,1)S(1)}, bf16[120,360]{1,0:T(8,128)(2,1)S(1)}, u32[]{:S(2)}, u32[]{:S(2)}) collective-permute-start(bf16[120,360]{1,0:T(8,128)(2,1)S(1)} %get-tuple-element.100), channel_id=1, source_target_pairs={{0,8},{8,0},{16,24},{24,16},{1,9},{9,1},{17,25},{25,17},{2,10},{10... | collective-permute-start | bytes 259208 | tf_op jit(solution)/shard_map/ppermute | solution.py:33
  67.3 15.1 %collective-permute-start.23 = (bf16[120,360]{1,0:T(8,128)(2,1)S(1)}, bf16[120,360]{1,0:T(8,128)(2,1)S(1)}, u32[]{:S(2)}, u32[]{:S(2)}) collective-permute-start(bf16[120,360]{1,0:T(8,128)(2,1)S(1)} %get-tuple-element.101), channel_id=1, source_target_pairs={{0,16},{8,24},{16,0},{24,8},{1,17},{9,25},{17,1},{25,9},{2,18},{10... | collective-permute-start | bytes 259208 | tf_op jit(solution)/shard_map/ppermute | solution.py:33
  69.6 12.8 %collective-permute-start.24 = (bf16[120,360]{1,0:T(8,128)(2,1)S(1)}, bf16[120,360]{1,0:T(8,128)(2,1)S(1)}, u32[]{:S(2)}, u32[]{:S(2)}) collective-permute-start(bf16[120,360]{1,0:T(8,128)(2,1)S(1)} %get-tuple-element.102), channel_id=1, source_target_pairs={{0,24},{8,16},{16,8},{24,0},{1,25},{9,17},{17,9},{25,1},{2,26},{10... | collective-permute-start | bytes 259208 | tf_op jit(solution)/shard_map/ppermute | solution.py:33
  71.7 9.4 %collective-permute-start.9 = (bf16[320,128]{1,0:T(8,128)(2,1)S(1)}, bf16[320,128]{1,0:T(8,128)(2,1)S(1)}, u32[]{:S(2)}, u32[]{:S(2)}) collective-permute-start(bf16[320,128]{1,0:T(8,128)(2,1)S(1)} %get-tuple-element.81), channel_id=1, source_target_pairs={{0,16},{8,24},{16,0},{24,8},{1,17},{9,25},{17,1},{25,9},{2,18},{10... | collective-permute-start | bytes 245768 | tf_op jit(solution)/shard_map/ppermute | solution.py:33
  71.7 9.4 %collective-permute-start.10 = (bf16[320,128]{1,0:T(8,128)(2,1)S(1)}, bf16[320,128]{1,0:T(8,128)(2,1)S(1)}, u32[]{:S(2)}, u32[]{:S(2)}) collective-permute-start(bf16[320,128]{1,0:T(8,128)(2,1)S(1)} %get-tuple-element.82), channel_id=1, source_target_pairs={{0,24},{8,16},{16,8},{24,0},{1,25},{9,17},{17,9},{25,1},{2,26},{10... | collective-permute-start | bytes 245768 | tf_op jit(solution)/shard_map/ppermute | solution.py:33
